TPU v7x, 256 devices: a whole 4x4x8 slice. The times are simulated.
256 devices in a mesh: tm: 128 (over z_lo, x, y, core), chan: 2 (over z_hi).
Axes of the slice: x: 4, y: 4, z: 8 (z_hi: 2, z_lo: 4; z = z_hi * 4 + z_lo), core: 2. Of those that a mesh axis runs over, the one named last changes fastest.
Arguments:
- spectrum: float32 [256, 131072], P('tm', 'chan'), may hold values from -6 to 6
- offsets: int32 [512], replicated, may hold values from 0 to 128, as said below
Outputs:
- peak: float32 [131072], P('chan')
Inputs may be any that keep to these rules, and one draw needn't show every extreme that they name: `offsets`: entries 0 and 1 are 0; entry 2L + d (drift d of the section that joins blocks of L) lies in 0 to L, and is exactly L for d = 2L - 1.
All inputs are finite; a program needn't handle non-finite values.
Results may differ from a plain program's by a relative error of at most 0.00002.
Values sent between devices are 32-bit elements; how exact they have to be, the bound alone decides.
No kernel may reach another device: no remote copies, remote signals or barrier semaphores. Data moves between devices by JAX's collectives and lax.ppermute only.
A program may use at most 64 MiB of HBM per device.

v0:
```python
import jax
import jax.numpy as jnp
from jax import lax
from jax.sharding import PartitionSpec as P


def shifted(value, axis, by):
    size = lax.axis_size(axis)
    pairs = [(i, i + by) for i in range(size) if 0 <= i + by < size]
    return lax.ppermute(value, axis, pairs)


def from_partner(value, axis, apart):
    return lax.ppermute(value, axis, [(i, i ^ 1 << apart) for i in range(lax.axis_size(axis))])


def take_window(single, amount, span_cols):
    return lax.dynamic_slice_in_dim(single, amount, span_cols)


def combine(lower_rows, upper_ext, shifts, span_cols):
    upper_two = jnp.repeat(upper_ext, 2, axis=0)
    moved = jax.vmap(take_window, in_axes=(0, 0, None))(upper_two, shifts, span_cols)
    return jnp.repeat(lower_rows, 2, axis=0) + moved


def lookup(offsets, table_ids, wanted):
    picked = jnp.where(table_ids[None, :] == wanted[:, None], offsets[None, :], 0)
    return jnp.sum(picked, axis=1)


def local(spectrum, offsets):
    rows_dev = spectrum.shape[0]
    span_cols = spectrum.shape[1]
    tm_count = lax.axis_size("tm")
    my_index = lax.axis_index("tm")
    table_ids = jnp.arange(offsets.shape[0], dtype=jnp.int32)

    def extend(upper_rows, width):
        edge = shifted(upper_rows[:, :width], "chan", -1)
        return jnp.concatenate([upper_rows, edge], axis=1)

    sums = spectrum
    length = 1
    while length < rows_dev:
        blocks = rows_dev // (2 * length)
        paired = sums.reshape(blocks, 2, length, span_cols)
        lower_rows = paired[:, 0].reshape(blocks * length, span_cols)
        upper_rows = paired[:, 1].reshape(blocks * length, span_cols)
        shifts = jnp.tile(offsets[2 * length : 4 * length], blocks)
        sums = combine(lower_rows, extend(upper_rows, length), shifts, span_cols)
        length = length * 2
    drifts = jnp.arange(rows_dev, dtype=jnp.int32)
    half = rows_dev // 2
    for bit_pos in range(tm_count.bit_length() - 1):
        length = rows_dev * 2**bit_pos
        is_low = my_index // 2**bit_pos % 2 == 0
        outgoing = jnp.where(is_low, sums[half:], sums[:half])
        incoming = from_partner(outgoing, "tm", bit_pos)
        lower_rows = jnp.where(is_low, sums[:half], incoming)
        upper_rows = jnp.where(is_low, incoming, sums[half:])
        kept = jnp.where(is_low, drifts[:half], drifts[half:])
        drifts = jnp.stack([2 * kept, 2 * kept + 1], axis=1).reshape(rows_dev)
        shifts = lookup(offsets, table_ids, 2 * length + drifts)
        sums = combine(lower_rows, extend(upper_rows, length), shifts, span_cols)
    return lax.pmax(jnp.max(sums, axis=0), "tm")


def solution(mesh):
    placed = (P("tm", "chan"), P())
    return jax.shard_map(local, mesh=mesh, in_specs=placed, out_specs=P("chan"), check_vma=False)
```

profile of v0, /device:TPU:1, one launch (start us, length us, event | category | flops | bytes accessed | tf_op | source)
XLA Modules:
  0.0 1433.8 jit_solution(1436587355535879024)
XLA Ops:
  13.5 5.6 collective-permute-done
  20.6 11.6 while.8
  21.3 1.9 dynamic-slice.49
  23.2 3.3 dynamic-update-slice.24
  27.1 1.9 dynamic-slice.49
  29.0 3.3 dynamic-update-slice.24
  32.8 2.7 collective-permute-start.1
  38.4 6.9 collective-permute-done.2
  46.4 11.6 while.9
  47.0 1.9 dynamic-slice.51
  48.9 3.3 dynamic-update-slice.25
  52.8 1.9 dynamic-slice.51
  54.7 3.3 dynamic-update-slice.25
  59.0 6.0 collective-permute-done.3
  66.8 6.9 collective-permute-done.4
  74.7 11.4 while.10
  77.1 3.3 dynamic-update-slice.26
  82.8 3.3 dynamic-update-slice.26
  86.7 2.1 collective-permute-start.5
  88.9 4.8 collective-permute-done.5
  95.4 6.9 collective-permute-done.6
  103.4 11.6 while.11
  104.1 1.9 dynamic-slice.55
  105.9 3.3 dynamic-update-slice.27
  109.8 1.9 dynamic-slice.55
  111.7 3.3 dynamic-update-slice.27
  115.8 5.1 collective-permute-done.7
  122.7 6.8 collective-permute-done.8
  130.6 11.5 while.12
  133.1 3.3 dynamic-update-slice.28
  138.8 3.3 dynamic-update-slice.28
  144.4 5.0 collective-permute-done.9
  151.3 6.8 collective-permute-done.10
  159.2 11.3 while.13
  161.6 3.3 dynamic-update-slice.29
  167.3 3.3 dynamic-update-slice.29
  171.2 5.2 collective-permute-done.11
  178.5 6.6 collective-permute-done.12
  186.2 11.6 while.14
  186.9 1.9 dynamic-slice.61
  188.7 3.3 dynamic-update-slice.30
  194.5 3.3 dynamic-update-slice.30
  199.9 7.5 collective-permute-done.13
  209.2 6.9 collective-permute-done.14
  217.2 11.6 while.15
  219.8 3.3 dynamic-update-slice.31
  225.6 3.3 dynamic-update-slice.31
  230.5 1194.7 %all-reduce.2.cloned.1.call-done = f32[65536]{0:T(1024)} async-done(((f32[65536]{0:T(1024)}), f32[65536]{0:T(1024)}) %all-reduce.2.cloned.1.call-update) | async-done | bytes 262160 | tf_op jit(solution)/shard_map/pmax | solution.py:66
  (141 shorter events, 66.6 us)
Async XLA Ops:
  6.5 1418.7 %all-reduce.2.cloned.1.call-start = ((), (), s32[]{:S(2)}) async-start(), calls=%async_computation | async-start | bytes 524288 | tf_op jit(solution)/shard_map/pmax | solution.py:66
  8.9 10.1 collective-permute-start
  11.7 0.7 copy-start
  32.8 3.9 collective-permute-start.1
  37.1 8.2 collective-permute-start.2
  58.6 6.4 collective-permute-start.3
  65.5 8.2 collective-permute-start.4
  86.7 7.0 collective-permute-start.5
  94.1 8.2 collective-permute-start.6
  115.5 5.3 collective-permute-start.7
  121.3 8.2 collective-permute-start.8
  142.7 6.8 collective-permute-start.9
  149.9 8.2 collective-permute-start.10
  171.1 5.3 collective-permute-start.11
  176.9 8.2 collective-permute-start.12
  198.4 9.0 collective-permute-start.13
  207.9 8.3 collective-permute-start.14
Sparse Core Ops, SparseCore 0:
  230.7 1194.5 all-reduce.1
where the time goes:
time: 1430 us
  waiting for transfers between devices  1280 us (90%)
  local copies, waits for them, and re-layouts  100 us (7%)
  starting transfers between devices  19.3 us (1%)
  other arithmetic  15.8 us (1%)
  between operations  14.9 us (1%)
    pmax x1, waiting for transfers between devices, local(): return lax.pmax(jnp.max(sums, axis=0), 'tm')  1190 us
    gather x64, local copies, waits for them, and re-layouts  91.7 us
    ppermute x8, waiting for transfers between devices, shifted(): return lax.ppermute(value, axis, pairs)  53.5 us
    ppermute x7, waiting for transfers between devices, from_partner(): lax.ppermute(value, axis, [(i, i ^ 1 << apart) for i in range(lax.axis_si...  34.7 us
  transfers between devices with their start and end apart: 16, of which 16 were waited for; matrix products, arithmetic and copies ran while one was open for 0% of the time, Pallas kernels for 0%

commit v1 on v0

v1 whole, which is shorter than its diff:
```python
import functools

import jax
import jax.numpy as jnp
from jax import lax
from jax.experimental import pallas as pl
from jax.experimental.pallas import tpu as pltpu
from jax.sharding import PartitionSpec as P

LANES = 128


def tree_kernel(total, cols, halo_cols, copies, offs_ref, main_ref, halo_ref, out_ref, a_ref, b_ref):
    lane = lax.broadcasted_iota(jnp.int32, (8, LANES), 1)
    pairs = total // 2
    tail = jnp.zeros((8 - cols - halo_cols, LANES), jnp.float32)

    def fetch(i, _):
        t = i // 2
        r = i % 2
        head = main_ref[pl.ds(t * (2 * cols) + r, cols, stride=2), :]
        more = halo_ref[pl.ds(t * (2 * halo_cols) + r, halo_cols, stride=2), :]
        a_ref[i] = jnp.concatenate([head, more, tail], axis=0)
        return _

    lax.fori_loop(0, total, fetch, 0, unroll=8)

    def moved(upper, amount):
        turned = pltpu.roll(upper, (LANES - amount) & (LANES - 1), axis=1)
        return jnp.where(lane < LANES - amount, turned, pltpu.roll(turned, 7, axis=0))

    src, dst = a_ref, b_ref
    length = 1
    while length < total // 2:
        blocks = total // (2 * length)

        def level(k, _, src=src, dst=dst, length=length, blocks=blocks):
            p = k // blocks
            b = k % blocks
            lower = src[2 * b * length + p]
            upper = src[(2 * b + 1) * length + p]
            for odd in range(2):
                d = 2 * p + odd
                amount = offs_ref[2 * length + d]
                dst[b * 2 * length + d] = lower + moved(upper, amount)
            return _

        lax.fori_loop(0, pairs, level, 0, unroll=8)
        src, dst = dst, src
        length *= 2

    def last(p, best):
        lower = src[p]
        upper = src[length + p]
        for odd in range(2):
            amount = offs_ref[2 * length + 2 * p + odd]
            best = jnp.maximum(best, lower + moved(upper, amount))
        return best

    best = lax.fori_loop(0, length, last, jnp.full((8, LANES), -jnp.inf, jnp.float32), unroll=8)
    for k in range(copies):
        out_ref[pl.ds(k * cols, cols), :] = best[:cols]


def to_previous(count, groups):
    place = [q % count * groups + q // count for q in range(count * groups)]
    return list(zip(place[1:], place))


def local(spectrum, offsets):
    rows, span = spectrum.shape
    count = lax.axis_size("tm")
    groups = lax.axis_size("chan")
    total = rows * count
    cols = span // count // LANES
    halo_cols = -(-(total - 1) // LANES)
    tiles = spectrum.reshape(rows, span // LANES, LANES).transpose(1, 0, 2)
    main = lax.all_to_all(tiles, "tm", 0, 0, tiled=True)
    edge = main.reshape(count, cols, rows, LANES)[:, :halo_cols]
    halo = lax.ppermute(edge, ("tm", "chan"), to_previous(count, groups))
    best = pl.pallas_call(
        functools.partial(tree_kernel, total, cols, halo_cols, count),
        out_shape=jax.ShapeDtypeStruct((count * cols, LANES), jnp.float32),
        in_specs=[
            pl.BlockSpec(memory_space=pltpu.SMEM),
            pl.BlockSpec(memory_space=pltpu.VMEM),
            pl.BlockSpec(memory_space=pltpu.VMEM),
        ],
        out_specs=pl.BlockSpec(memory_space=pltpu.VMEM),
        scratch_shapes=[pltpu.VMEM((total, 8, LANES), jnp.float32)] * 2,
    )(offsets, main.reshape(-1, LANES), halo.reshape(-1, LANES))
    peak = lax.all_to_all(best, "tm", 0, 0, tiled=True)
    return peak.reshape(span)


def solution(mesh):
    placed = (P("tm", "chan"), P())
    return jax.shard_map(local, mesh=mesh, in_specs=placed, out_specs=P("chan"), check_vma=False)
```

time: 1430 us -> 85.3 us (0.06)
  waiting for transfers between devices: 1280 us -> 4.51 us
  local copies, waits for them, and re-layouts: 100 us -> 1.47 us
  blocking collectives: 0 us -> 55.7 us
  Pallas kernels: 0 us -> 20.2 us
  starting transfers between devices: 19.3 us -> 3.17 us
  other arithmetic: 15.8 us -> 0 us
  between operations: 14.9 us -> 0.02 us
    pmax x1 -> x0, waiting for transfers between devices: 1190 us -> none  [local(): return lax.pmax(jnp.max(sums, axis=0), 'tm')]
    gather x64 -> x0, local copies, waits for them, and re-layouts: 91.7 us -> none
    ppermute x15 -> x1, waiting for transfers between devices: 88.1 us -> 4.51 us  [local(): halo = lax.ppermute(edge, ('tm', 'chan'), to_previous(count, groups))]
    all_to_all x0 -> x2, blocking collectives: none -> 55.7 us  [the longest x1 32 us: local(): main = lax.all_to_all(tiles, 'tm', 0, 0, tiled=True)]
    pallas_call x0 -> x1, Pallas kernels: none -> 20.2 us  [local(): pl.pallas_call(functools.partial(tree_kernel, total, cols, halo_cols, cou...]
    ppermute x15 -> x1, starting transfers between devices: 19.3 us -> 3.17 us  [local(): halo = lax.ppermute(edge, ('tm', 'chan'), to_previous(count, groups))]
  transfers between devices with their start and end apart: 16 -> 1, of which waited for: 16 -> 1; matrix products, arithmetic and copies ran while one was open for 0% -> 0% of each run, Pallas kernels for 0% -> 0%
where the time goes in v1:
time: 85.3 us; the launch traced here: 85.1 us
  blocking collectives  55.7 us (65%)
  Pallas kernels  20.2 us (24%)
  waiting for transfers between devices  4.51 us (5%)
  starting transfers between devices  3.17 us (4%)
  local copies, waits for them, and re-layouts  1.47 us (2%)
    all_to_all x1, blocking collectives, local(): main = lax.all_to_all(tiles, 'tm', 0, 0, tiled=True)  32 us
    all_to_all x1, blocking collectives, local(): peak = lax.all_to_all(best, 'tm', 0, 0, tiled=True)  23.7 us
    pallas_call x1, Pallas kernels, local(): pl.pallas_call(functools.partial(tree_kernel, total, cols, halo_cols, cou...  20.2 us
    ppermute x1, waiting for transfers between devices, local(): halo = lax.ppermute(edge, ('tm', 'chan'), to_previous(count, groups))  4.51 us
    ppermute x1, starting transfers between devices, local(): halo = lax.ppermute(edge, ('tm', 'chan'), to_previous(count, groups))  3.17 us
  transfers between devices with their start and end apart: 1, of which 1 were waited for; matrix products, arithmetic and copies ran while one was open for 0% of the time, Pallas kernels for 0%

profile of v1, /device:TPU:1, one launch (start us, length us, event | category | flops | bytes accessed | tf_op | source)
XLA Modules:
  0.0 85.1 jit_solution(3667866507100985253)
XLA Ops:
  0.0 32.0 %all_to_all.14 = f32[512,2,128]{2,1,0:T(2,128)S(1)} all-to-all(f32[512,2,128]{2,1,0:T(2,128)} %bitcast.12), channel_id=1, replica_groups=mesh['tm'=128,'chan'=2] {'tm'}, dimensions={0} | all-to-all | bytes 1048576 | tf_op jit(solution)/shard_map/all_to_all | solution.py:78
  32.0 0.0 copy-start
  32.1 3.2 %collective-permute-start = (f32[128,2,2,128]{3,2,1,0:T(2,128)S(1)}, f32[128,2,2,128]{3,2,1,0:T(2,128)S(1)}, u32[]{:S(2)}, u32[]{:S(2)}) collective-permute-start(f32[128,2,2,128]{3,2,1,0:T(2,128)S(1)} %slice.4), channel_id=1, source_target_pairs={{2,0},{4,2},{6,4},{8,6},{10,8},{12,10},{14,12},{16,14},{18,16},{20... | collective-permute-start | bytes 786440 | tf_op jit(solution)/shard_map/ppermute | solution.py:80
  35.2 4.5 %collective-permute-done = f32[128,2,2,128]{3,2,1,0:T(2,128)S(1)} collective-permute-done((f32[128,2,2,128]{3,2,1,0:T(2,128)S(1)}, f32[128,2,2,128]{3,2,1,0:T(2,128)S(1)}, u32[]{:S(2)}, u32[]{:S(2)}) %collective-permute-start) | collective-permute-done | bytes 262176 | tf_op jit(solution)/shard_map/ppermute | solution.py:80
  39.8 0.0 copy-start.1
  39.8 0.0 copy-done
  39.8 0.7 copy-done.1
  40.5 20.2 %shard_map.28 = f32[512,128]{1,0:T(8,128)} custom-call(s32[512]{0:T(512)} %offs_ref.1, f32[1024,128]{1,0:T(8,128)} %bitcast.9, f32[512,128]{1,0:T(8,128)} %bitcast.13), custom_call_target="tpu_custom_call" | custom-call | tf_op jit(solution)/shard_map/pallas_call | solution.py:81
  60.7 23.7 %all_to_all.15 = f32[128,4,128]{2,1,0:T(4,128)S(1)} all-to-all(f32[128,4,128]{2,1,0:T(4,128)} %bitcast.11), channel_id=1, replica_groups=mesh['tm'=128,'chan'=2] {'tm'}, dimensions={0} | all-to-all | bytes 524288 | tf_op jit(solution)/shard_map/all_to_all | solution.py:92
  84.4 0.7 copy.5
  (1 shorter events, 0.0 us)
Async XLA Ops:
  32.0 7.7 %copy-start = (f32[512,2,128]{2,1,0:T(2,128)}, f32[512,2,128]{2,1,0:T(2,128)S(1)}, u32[]{:S(2)}) copy-start(f32[512,2,128]{2,1,0:T(2,128)S(1)} %all_to_all.14) | copy-start | bytes 1572868
  32.1 7.7 %collective-permute-start = (f32[128,2,2,128]{3,2,1,0:T(2,128)S(1)}, f32[128,2,2,128]{3,2,1,0:T(2,128)S(1)}, u32[]{:S(2)}, u32[]{:S(2)}) collective-permute-start(f32[128,2,2,128]{3,2,1,0:T(2,128)S(1)} %slice.4), channel_id=1, source_target_pairs={{2,0},{4,2},{6,4},{8,6},{10,8},{12,10},{14,12},{16,14},{18,16},{20... | collective-permute-start | bytes 786440 | tf_op jit(solution)/shard_map/ppermute | solution.py:80
  39.8 0.7 copy-start.1

commit v2 on v1

v2 whole, which is shorter than its diff:
```python
import functools

import jax
import jax.numpy as jnp
from jax import lax
from jax.experimental import pallas as pl
from jax.experimental.pallas import tpu as pltpu
from jax.sharding import PartitionSpec as P

LANES = 128
VMEM_LIMIT = 6 * 2**20


def sublanes():
    return lax.broadcasted_iota(jnp.int32, (8, LANES), 0)


def moved(upper, amount):
    lane = lax.broadcasted_iota(jnp.int32, (8, LANES), 1)
    turned = pltpu.roll(upper, (LANES - amount) & (LANES - 1), axis=1)
    return jnp.where(lane < LANES - amount, turned, pltpu.roll(turned, 7, axis=0))


def tree(offs_ref, get, total, a_ref, b_ref):
    half = total // 2
    for q in range(half // 2):
        lower, upper = get(q, 0), get(q, 1)
        for d in range(2):
            b_ref[2 * q + d] = lower + moved(upper, offs_ref[2 + d])
    src, dst = b_ref, a_ref
    length = 2
    while length < half:
        for p in range(length):
            amounts = [offs_ref[2 * length + 2 * p + odd] for odd in range(2)]
            for b in range(half // (2 * length)):
                lower = src[2 * b * length + p]
                upper = src[(2 * b + 1) * length + p]
                for odd in range(2):
                    dst[b * 2 * length + 2 * p + odd] = lower + moved(upper, amounts[odd])
        src, dst = dst, src
        length *= 2
    first = sublanes() < 4
    best = [jnp.full((8, LANES), -jnp.inf, jnp.float32) for _ in range(4)]
    for p in range(half):
        both = src[p]
        other = pltpu.roll(both, 4, axis=0)
        lower = jnp.where(first, both, other)
        even = moved(other, offs_ref[2 * length + 2 * p])
        odd = moved(both, offs_ref[2 * length + 2 * p + 1])
        best[p % 4] = jnp.maximum(best[p % 4], lower + jnp.where(first, even, odd))
    peak = functools.reduce(jnp.maximum, best)
    return jnp.maximum(peak, pltpu.roll(peak, 4, axis=0))


def near_kernel(total, offs_ref, main_ref, out_ref, a_ref, b_ref):
    half = total // 4

    def get(t, r):
        one = main_ref[pl.ds(t * 8 + r, 8, stride=2), :]
        two = main_ref[pl.ds((t + half - 1) * 8 + r, 8, stride=2), :]
        return jnp.where(sublanes() < 4, one, two)

    out_ref[...] = tree(offs_ref, get, total, a_ref, b_ref)


def far_kernel(total, copies, offs_ref, main_ref, halo_ref, near_ref, out_ref, a_ref, b_ref):
    half = total // 4
    sub = sublanes()

    def get(t, r):
        head_one = main_ref[pl.ds(t * 8 + r + 4, 2, stride=2), :]
        head_two = main_ref[pl.ds((t + half) * 8 + r + 4, 2, stride=2), :]
        tail_one = halo_ref[pl.ds(t * 4 + r, 2, stride=2), :]
        tail_two = halo_ref[pl.ds((t + half) * 4 + r, 2, stride=2), :]
        return jnp.concatenate([head_one, tail_one, head_two, tail_two], axis=0)

    far = tree(offs_ref, get, total, a_ref, b_ref)
    both = jnp.where(sub % 4 < 2, near_ref[...], pltpu.roll(far, 2, axis=0))
    for k in range(copies // 2):
        out_ref[pl.ds(k * 8, 8), :] = both


def to_previous(count, groups):
    place = [q % count * groups + q // count for q in range(count * groups)]
    return list(zip(place[1:], place))


def local(spectrum, offsets):
    rows, span = spectrum.shape
    count = lax.axis_size("tm")
    groups = lax.axis_size("chan")
    total = rows * count
    cols = span // count // LANES
    tiles = spectrum.reshape(rows, span // LANES, LANES).transpose(1, 0, 2)
    main = lax.all_to_all(tiles, "tm", 0, 0, tiled=True)
    edge = main.reshape(count, cols, rows, LANES)[:, : cols // 2]
    halo = lax.ppermute(edge, ("tm", "chan"), to_previous(count, groups))
    main = main.reshape(-1, LANES)
    smem = pl.BlockSpec(memory_space=pltpu.SMEM)
    vmem = pl.BlockSpec(memory_space=pltpu.VMEM)
    scratch = [pltpu.VMEM((total // 2, 8, LANES), jnp.float32)] * 2
    params = pltpu.CompilerParams(vmem_limit_bytes=VMEM_LIMIT)
    cost = pl.CostEstimate(flops=20_000_000, bytes_accessed=600_000, transcendentals=0)
    near = pl.pallas_call(
        functools.partial(near_kernel, total),
        out_shape=jax.ShapeDtypeStruct((8, LANES), jnp.float32),
        in_specs=[smem, vmem],
        out_specs=vmem,
        scratch_shapes=scratch,
        compiler_params=params,
        cost_estimate=cost,
    )(offsets, main)
    best = pl.pallas_call(
        functools.partial(far_kernel, total, count),
        out_shape=jax.ShapeDtypeStruct((count * cols, LANES), jnp.float32),
        in_specs=[smem, vmem, vmem, vmem],
        out_specs=vmem,
        scratch_shapes=scratch,
        compiler_params=params,
        cost_estimate=cost,
    )(offsets, main, halo.reshape(-1, LANES), near)
    peak = lax.all_to_all(best, "tm", 0, 0, tiled=True)
    return peak.reshape(span)


def solution(mesh):
    placed = (P("tm", "chan"), P())
    return jax.shard_map(local, mesh=mesh, in_specs=placed, out_specs=P("chan"), check_vma=False)
```

time: 85.3 us -> 66.2 us (0.78)
  Pallas kernels: 20.2 us -> 4.03 us
  waiting for transfers between devices: 4.51 us -> 2.5 us
    pallas_call x1 -> x2, Pallas kernels: 20.2 us -> 4.03 us  [the longest x1 2.04 us: local(): pl.pallas_call(functools.partial(far_kernel, total, count), out_shape=jax...]
    ppermute x1, waiting for transfers between devices: 4.51 us -> 2.5 us  [local(): halo = lax.ppermute(edge, ('tm', 'chan'), to_previous(count, groups))]
  transfers between devices with their start and end apart: 1 -> 1, of which waited for: 1 -> 1; matrix products, arithmetic and copies ran while one was open for 0% -> 0% of each run, Pallas kernels for 0% -> 3%
where the time goes in v2:
time: 66.2 us; the launch traced here: 66 us
  blocking collectives  55.5 us (84%)
  Pallas kernels  4.03 us (6%)
  starting transfers between devices  3.17 us (5%)
  waiting for transfers between devices  2.5 us (4%)
  local copies, waits for them, and re-layouts  0.77 us (1%)
    all_to_all x1, blocking collectives, local(): main = lax.all_to_all(tiles, 'tm', 0, 0, tiled=True)  32 us
    all_to_all x1, blocking collectives, local(): peak = lax.all_to_all(best, 'tm', 0, 0, tiled=True)  23.5 us
    ppermute x1, starting transfers between devices, local(): halo = lax.ppermute(edge, ('tm', 'chan'), to_previous(count, groups))  3.17 us
    ppermute x1, waiting for transfers between devices, local(): halo = lax.ppermute(edge, ('tm', 'chan'), to_previous(count, groups))  2.5 us
    pallas_call x1, Pallas kernels, local(): pl.pallas_call(functools.partial(far_kernel, total, count), out_shape=jax...  2.04 us
    pallas_call x1, Pallas kernels, local(): pl.pallas_call(functools.partial(near_kernel, total), out_shape=jax.Shape...  2 us
  transfers between devices with their start and end apart: 1, of which 1 were waited for; matrix products, arithmetic and copies ran while one was open for 0% of the time, Pallas kernels for 3%

profile of v2, /device:TPU:1, one launch (start us, length us, event | category | flops | bytes accessed | tf_op | source)
XLA Modules:
  0.0 66.0 jit_solution(1280108265715416255)
XLA Ops:
  0.0 32.0 %all_to_all.14 = f32[512,2,128]{2,1,0:T(2,128)S(1)} all-to-all(f32[512,2,128]{2,1,0:T(2,128)} %bitcast.14), channel_id=1, replica_groups=mesh['tm'=128,'chan'=2] {'tm'}, dimensions={0} | all-to-all | bytes 1048576 | tf_op jit(solution)/shard_map/all_to_all | solution.py:95
  32.0 0.0 copy-start
  32.1 3.2 %collective-permute-start = (f32[128,2,2,128]{3,2,1,0:T(2,128)S(1)}, f32[128,2,2,128]{3,2,1,0:T(2,128)S(1)}, u32[]{:S(2)}, u32[]{:S(2)}) collective-permute-start(f32[128,2,2,128]{3,2,1,0:T(2,128)S(1)} %slice.4), channel_id=1, source_target_pairs={{2,0},{4,2},{6,4},{8,6},{10,8},{12,10},{14,12},{16,14},{18,16},{20... | collective-permute-start | bytes 786440 | tf_op jit(solution)/shard_map/ppermute | solution.py:97
  35.2 0.0 copy-done
  35.2 2.0 %shard_map.28.near_ref = f32[8,128]{1,0:T(8,128)S(1)} custom-call(s32[512]{0:T(512)S(1)} %copy-done, f32[1024,128]{1,0:T(8,128)S(1)} %bitcast.9), custom_call_target="tpu_custom_call" | custom-call | flops 20000000 | bytes 600000 | tf_op jit(solution)/shard_map/pallas_call | solution.py:104
  37.3 2.5 %collective-permute-done = f32[128,2,2,128]{3,2,1,0:T(2,128)S(1)} collective-permute-done((f32[128,2,2,128]{3,2,1,0:T(2,128)S(1)}, f32[128,2,2,128]{3,2,1,0:T(2,128)S(1)}, u32[]{:S(2)}, u32[]{:S(2)}) %collective-permute-start) | collective-permute-done | bytes 262176 | tf_op jit(solution)/shard_map/ppermute | solution.py:97
  39.8 2.0 %shard_map.29 = f32[512,128]{1,0:T(8,128)S(1)} custom-call(s32[512]{0:T(512)S(1)} %copy-done, f32[1024,128]{1,0:T(8,128)S(1)} %bitcast.10, f32[512,128]{1,0:T(8,128)S(1)} %bitcast.12, f32[8,128]{1,0:T(8,128)S(1)} %shard_map.28.near_ref), custom_call_target="tpu_custom_call" | custom-call | flops 20000000 | bytes 600000 | tf_op jit(solution)/shard_map/pallas_call | solution.py:113
  41.8 23.5 %all_to_all.15 = f32[128,4,128]{2,1,0:T(4,128)S(1)} all-to-all(f32[128,4,128]{2,1,0:T(4,128)S(1)} %bitcast.11), channel_id=1, replica_groups=mesh['tm'=128,'chan'=2] {'tm'}, dimensions={0} | all-to-all | bytes 524288 | tf_op jit(solution)/shard_map/all_to_all | solution.py:122
  65.3 0.7 %copy.5 = f32[65536]{0:T(1024)} copy(f32[65536]{0:T(1024)S(1)} %bitcast.13) | data formatting | bytes 524288
  (1 shorter events, 0.0 us)
Async XLA Ops:
  32.0 3.2 %copy-start = (s32[512]{0:T(512)S(1)}, s32[512]{0:T(512)}, u32[]{:S(2)}) copy-start(s32[512]{0:T(512)} %offs_ref.3) | copy-start | bytes 6148
  32.1 7.7 %collective-permute-start = (f32[128,2,2,128]{3,2,1,0:T(2,128)S(1)}, f32[128,2,2,128]{3,2,1,0:T(2,128)S(1)}, u32[]{:S(2)}, u32[]{:S(2)}) collective-permute-start(f32[128,2,2,128]{3,2,1,0:T(2,128)S(1)} %slice.4), channel_id=1, source_target_pairs={{2,0},{4,2},{6,4},{8,6},{10,8},{12,10},{14,12},{16,14},{18,16},{20... | collective-permute-start | bytes 786440 | tf_op jit(solution)/shard_map/ppermute | solution.py:97

commit v3 on v2

--- a/solution.py
+++ b/solution.py
@@ -52,27 +52,30 @@
     return jnp.maximum(peak, pltpu.roll(peak, 4, axis=0))
 
 
-def near_kernel(total, offs_ref, main_ref, out_ref, a_ref, b_ref):
+def near_kernel(total, spot, offs_ref, main_ref, out_ref, a_ref, b_ref):
     half = total // 4
 
     def get(t, r):
-        one = main_ref[pl.ds(t * 8 + r, 8, stride=2), :]
-        two = main_ref[pl.ds((t + half - 1) * 8 + r, 8, stride=2), :]
-        return jnp.where(sublanes() < 4, one, two)
+        one = main_ref[pl.ds(spot[t] * 8 + r, 4, stride=2), :]
+        two = main_ref[pl.ds(spot[t + half] * 8 + r, 4, stride=2), :]
+        return jnp.concatenate([one, two], axis=0)
 
     out_ref[...] = tree(offs_ref, get, total, a_ref, b_ref)
 
 
-def far_kernel(total, copies, offs_ref, main_ref, halo_ref, near_ref, out_ref, a_ref, b_ref):
+def far_kernel(total, copies, spot, offs_ref, more_ref, main_ref, halo_ref, near_ref, out_ref, a_ref, b_ref):
     half = total // 4
     sub = sublanes()
+    keep = (sub % 4 < 2) | (more_ref[0] > 0)
 
     def get(t, r):
-        head_one = main_ref[pl.ds(t * 8 + r + 4, 2, stride=2), :]
-        head_two = main_ref[pl.ds((t + half) * 8 + r + 4, 2, stride=2), :]
-        tail_one = halo_ref[pl.ds(t * 4 + r, 2, stride=2), :]
-        tail_two = halo_ref[pl.ds((t + half) * 4 + r, 2, stride=2), :]
-        return jnp.concatenate([head_one, tail_one, head_two, tail_two], axis=0)
+        one, two = spot[t], spot[t + half]
+        head_one = main_ref[pl.ds(one * 8 + r + 4, 2, stride=2), :]
+        head_two = main_ref[pl.ds(two * 8 + r + 4, 2, stride=2), :]
+        tail_one = halo_ref[pl.ds(one * 4 + r, 2, stride=2), :]
+        tail_two = halo_ref[pl.ds(two * 4 + r, 2, stride=2), :]
+        both = jnp.concatenate([head_one, tail_one, head_two, tail_two], axis=0)
+        return jnp.where(keep, both, 0.0)
 
     far = tree(offs_ref, get, total, a_ref, b_ref)
     both = jnp.where(sub % 4 < 2, near_ref[...], pltpu.roll(far, 2, axis=0))
@@ -80,9 +83,23 @@
         out_ref[pl.ds(k * 8, 8), :] = both
 
 
-def to_previous(count, groups):
-    place = [q % count * groups + q // count for q in range(count * groups)]
-    return list(zip(place[1:], place))
+def walk(count):
+    side, cores = 4, 2
+    plane = [(x, 0) for x in range(side)]
+    for y in range(1, side):
+        xs = range(1, side)
+        plane += [(x, y) for x in (xs[::-1] if y % 2 else xs)]
+    plane += [(0, y) for y in range(side - 1, 0, -1)]
+    order = []
+    for z in range(count // (side * side * cores)):
+        for x, y in plane if z % 2 == 0 else plane[::-1]:
+            order += [((z * side + x) * side + y) * cores + core for core in range(cores)]
+    return order
+
+
+def to_previous(order, groups):
+    place = [t * groups + g for g in range(groups) for t in order]
+    return list(zip(place, place[-1:] + place[:-1]))
 
 
 def local(spectrum, offsets):
@@ -91,10 +108,14 @@
     groups = lax.axis_size("chan")
     total = rows * count
     cols = span // count // LANES
+    order = walk(count)
+    spot = [order.index(t) for t in range(count)]
+    more = (lax.axis_index("tm") != order[-1]) | (lax.axis_index("chan") != groups - 1)
+    more = jnp.reshape(more, (1,)).astype(jnp.int32)
     tiles = spectrum.reshape(rows, span // LANES, LANES).transpose(1, 0, 2)
-    main = lax.all_to_all(tiles, "tm", 0, 0, tiled=True)
+    main = lax.all_to_all(tiles, "tm", 0, 0, axis_index_groups=[order], tiled=True)
     edge = main.reshape(count, cols, rows, LANES)[:, : cols // 2]
-    halo = lax.ppermute(edge, ("tm", "chan"), to_previous(count, groups))
+    halo = lax.ppermute(edge, ("tm", "chan"), to_previous(order, groups))
     main = main.reshape(-1, LANES)
     smem = pl.BlockSpec(memory_space=pltpu.SMEM)
     vmem = pl.BlockSpec(memory_space=pltpu.VMEM)
@@ -102,7 +123,7 @@
     params = pltpu.CompilerParams(vmem_limit_bytes=VMEM_LIMIT)
     cost = pl.CostEstimate(flops=20_000_000, bytes_accessed=600_000, transcendentals=0)
     near = pl.pallas_call(
-        functools.partial(near_kernel, total),
+        functools.partial(near_kernel, total, spot),
         out_shape=jax.ShapeDtypeStruct((8, LANES), jnp.float32),
         in_specs=[smem, vmem],
         out_specs=vmem,
@@ -111,15 +132,15 @@
         cost_estimate=cost,
     )(offsets, main)
     best = pl.pallas_call(
-        functools.partial(far_kernel, total, count),
+        functools.partial(far_kernel, total, count, spot),
         out_shape=jax.ShapeDtypeStruct((count * cols, LANES), jnp.float32),
-        in_specs=[smem, vmem, vmem, vmem],
+        in_specs=[smem, smem, vmem, vmem, vmem],
         out_specs=vmem,
         scratch_shapes=scratch,
         compiler_params=params,
         cost_estimate=cost,
-    )(offsets, main, halo.reshape(-1, LANES), near)
-    peak = lax.all_to_all(best, "tm", 0, 0, tiled=True)
+    )(offsets, more, main, halo.reshape(-1, LANES), near)
+    peak = lax.all_to_all(best, "tm", 0, 0, axis_index_groups=[order], tiled=True)
     return peak.reshape(span)
 
 

time: 66.2 us -> 59.9 us (0.905)
  blocking collectives: 55.5 us -> 51 us
  starting transfers between devices: 3.17 us -> 1.34 us
  local copies, waits for them, and re-layouts: 0.77 us -> 1.45 us
    all_to_all x2, blocking collectives: 55.5 us -> 51 us  [the longest x1 32 us: local(): lax.all_to_all(tiles, 'tm', 0, 0, axis_index_groups=[order], tiled=True)]
    ppermute x1, starting transfers between devices: 3.17 us -> 1.34 us  [local(): halo = lax.ppermute(edge, ('tm', 'chan'), to_previous(order, groups))]
    unnamed x3, local copies, waits for them, and re-layouts: 0.72 us -> 1.4 us
where the time goes in v3:
time: 59.9 us; the launch traced here: 59.7 us
  blocking collectives  51 us (85%)
  Pallas kernels  4.02 us (7%)
  waiting for transfers between devices  1.86 us (3%)
  local copies, waits for them, and re-layouts  1.45 us (2%)
  starting transfers between devices  1.34 us (2%)
    all_to_all x1, blocking collectives, local(): lax.all_to_all(tiles, 'tm', 0, 0, axis_index_groups=[order], tiled=True)  32 us
    all_to_all x1, blocking collectives, local(): lax.all_to_all(best, 'tm', 0, 0, axis_index_groups=[order], tiled=True)  19 us
    pallas_call x1, Pallas kernels, local(): pl.pallas_call(functools.partial(far_kernel, total, count, spot), out_sha...  2.03 us
    pallas_call x1, Pallas kernels, local(): pl.pallas_call(functools.partial(near_kernel, total, spot), out_shape=jax...  1.99 us
    ppermute x1, waiting for transfers between devices, local(): halo = lax.ppermute(edge, ('tm', 'chan'), to_previous(order, groups))  1.86 us
    unnamed x3, local copies, waits for them, and re-layouts  1.4 us
    ppermute x1, starting transfers between devices, local(): halo = lax.ppermute(edge, ('tm', 'chan'), to_previous(order, groups))  1.34 us
  transfers between devices with their start and end apart: 1, of which 1 were waited for; matrix products, arithmetic and copies ran while one was open for 0% of the time, Pallas kernels for 3%

profile of v3, /device:TPU:1, one launch (start us, length us, event | category | flops | bytes accessed | tf_op | source)
XLA Modules:
  0.0 59.7 jit_solution(10755765969492204213)
XLA Ops:
  0.0 32.0 %all_to_all.14 = f32[512,2,128]{2,1,0:T(2,128)S(1)} all-to-all(f32[512,2,128]{2,1,0:T(2,128)} %bitcast.15), channel_id=1, replica_groups={{0,2,16,18,32,34,48,50,52,54,36,38,20,22,24,26,40,42,56,58,60,62,44,46,..., dimensions={0} | all-to-all | bytes 1048576 | tf_op jit(solution)/shard_map/all_to_all | solution.py:116
  32.1 1.3 %collective-permute-start = (f32[128,2,2,128]{3,2,1,0:T(2,128)S(1)}, f32[128,2,2,128]{3,2,1,0:T(2,128)S(1)}, u32[]{:S(2)}, u32[]{:S(2)}) collective-permute-start(f32[128,2,2,128]{3,2,1,0:T(2,128)S(1)} %slice.4), channel_id=1, source_target_pairs={{0,195},{2,0},{16,2},{18,16},{32,18},{34,32},{48,34},{50,48},{52,5... | collective-permute-start | bytes 786440 | tf_op jit(solution)/shard_map/ppermute | solution.py:118
  33.4 0.0 copy-start
  33.4 0.7 %copy-done = s32[512]{0:T(512)S(1)} copy-done((s32[512]{0:T(512)S(1)}, s32[512]{0:T(512)}, u32[]{:S(2)}) %copy-start) | copy-done | bytes 2072
  34.1 2.0 %shard_map.28.near_ref = f32[8,128]{1,0:T(8,128)S(1)} custom-call(s32[512]{0:T(512)S(1)} %copy-done, f32[1024,128]{1,0:T(8,128)S(1)} %bitcast.10), custom_call_target="tpu_custom_call" | custom-call | flops 20000000 | bytes 600000 | tf_op jit(solution)/shard_map/pallas_call | solution.py:125
  36.1 1.9 %collective-permute-done = f32[128,2,2,128]{3,2,1,0:T(2,128)S(1)} collective-permute-done((f32[128,2,2,128]{3,2,1,0:T(2,128)S(1)}, f32[128,2,2,128]{3,2,1,0:T(2,128)S(1)}, u32[]{:S(2)}, u32[]{:S(2)}) %collective-permute-start) | collective-permute-done | bytes 262176 | tf_op jit(solution)/shard_map/ppermute | solution.py:118
  37.9 2.0 %shard_map.29 = f32[512,128]{1,0:T(8,128)S(1)} custom-call(s32[512]{0:T(512)S(1)} %copy-done, s32[1]{0:T(128)} %bitcast.more_ref, f32[1024,128]{1,0:T(8,128)S(1)} %bitcast.11, f32[512,128]{1,0:T(8,128)S(1)} %bitcast.13, f32[8,128]{1,0:T(8,128)S(1)} %shard_map.28.near_ref), custom_call_target="tpu_custom_call" | custom-call | flops 20000000 | bytes 600000 | tf_op jit(solution)/shard_map/pallas_call | solution.py:134
  40.0 19.0 %all_to_all.15 = f32[128,4,128]{2,1,0:T(4,128)S(1)} all-to-all(f32[128,4,128]{2,1,0:T(4,128)S(1)} %bitcast.12), channel_id=1, replica_groups={{0,2,16,18,32,34,48,50,52,54,36,38,20,22,24,26,40,42,56,58,60,62,44,46,..., dimensions={0} | all-to-all | bytes 524288 | tf_op jit(solution)/shard_map/all_to_all | solution.py:143
  58.9 0.7 %copy.5 = f32[65536]{0:T(1024)} copy(f32[65536]{0:T(1024)S(1)} %bitcast.14) | data formatting | bytes 524288
  (1 shorter events, 0.0 us)
Async XLA Ops:
  32.1 5.9 %collective-permute-start = (f32[128,2,2,128]{3,2,1,0:T(2,128)S(1)}, f32[128,2,2,128]{3,2,1,0:T(2,128)S(1)}, u32[]{:S(2)}, u32[]{:S(2)}) collective-permute-start(f32[128,2,2,128]{3,2,1,0:T(2,128)S(1)} %slice.4), channel_id=1, source_target_pairs={{0,195},{2,0},{16,2},{18,16},{32,18},{34,32},{48,34},{50,48},{52,5... | collective-permute-start | bytes 786440 | tf_op jit(solution)/shard_map/ppermute | solution.py:118
  33.4 0.7 %copy-start = (s32[512]{0:T(512)S(1)}, s32[512]{0:T(512)}, u32[]{:S(2)}) copy-start(s32[512]{0:T(512)} %offs_ref.3) | copy-start | bytes 6148

commit v4 on v3

--- a/solution.py
+++ b/solution.py
@@ -132,16 +132,22 @@
         cost_estimate=cost,
     )(offsets, main)
     best = pl.pallas_call(
-        functools.partial(far_kernel, total, count, spot),
-        out_shape=jax.ShapeDtypeStruct((count * cols, LANES), jnp.float32),
+        functools.partial(far_kernel, total, count // 2, spot),
+        out_shape=jax.ShapeDtypeStruct((count // 2 * cols, LANES), jnp.float32),
         in_specs=[smem, smem, vmem, vmem, vmem],
         out_specs=vmem,
         scratch_shapes=scratch,
         compiler_params=params,
         cost_estimate=cost,
     )(offsets, more, main, halo.reshape(-1, LANES), near)
-    peak = lax.all_to_all(best, "tm", 0, 0, axis_index_groups=[order], tiled=True)
-    return peak.reshape(span)
+    cores = [order[core::2] for core in range(2)]
+    ours = lax.all_to_all(best, "tm", 0, 0, axis_index_groups=cores, tiled=True)
+    theirs = lax.ppermute(ours, "tm", [(t, t ^ 1) for t in range(count)])
+    pair = [part.reshape(count // 2, 1, cols, LANES) for part in (ours, theirs)]
+    second = lax.axis_index("tm") % 2 == 1
+    first_core = jnp.where(second, pair[1], pair[0])
+    second_core = jnp.where(second, pair[0], pair[1])
+    return jnp.concatenate([first_core, second_core], axis=1).reshape(span)
 
 
 def solution(mesh):

time: 59.9 us -> 57.5 us (0.960)
  blocking collectives: 51 us -> 47.1 us
  waiting for transfers between devices: 1.86 us -> 3.2 us
  other arithmetic: 0 us -> 0.81 us
  local copies, waits for them, and re-layouts: 1.45 us -> 0.73 us
    all_to_all x1, blocking collectives: 19 us -> 15.1 us  [local(): ours = lax.all_to_all(best, 'tm', 0, 0, axis_index_groups=cores, tiled=True)]
    ppermute x0 -> x1, waiting for transfers between devices: none -> 1.35 us  [local(): theirs = lax.ppermute(ours, 'tm', [(t, t ^ 1) for t in range(count)])]
    concatenate x0 -> x1, other arithmetic: none -> 0.76 us  [local(): return jnp.concatenate([first_core, second_core], axis=1).reshape(span)]
    unnamed x3 -> x2, local copies, waits for them, and re-layouts: 1.4 us -> 0.68 us
  transfers between devices with their start and end apart: 1 -> 2, of which waited for: 1 -> 2; matrix products, arithmetic and copies ran while one was open for 0% -> 0% of each run, Pallas kernels for 3% -> 3%
where the time goes in v4:
time: 57.5 us; the launch traced here: 57.2 us
  blocking collectives  47.1 us (82%)
  Pallas kernels  4.02 us (7%)
  waiting for transfers between devices  3.2 us (6%)
  starting transfers between devices  1.34 us (2%)
  other arithmetic  0.81 us (1%)
  local copies, waits for them, and re-layouts  0.73 us (1%)
    all_to_all x1, blocking collectives, local(): lax.all_to_all(tiles, 'tm', 0, 0, axis_index_groups=[order], tiled=True)  32 us
    all_to_all x1, blocking collectives, local(): ours = lax.all_to_all(best, 'tm', 0, 0, axis_index_groups=cores, tiled=True)  15.1 us
    pallas_call x1, Pallas kernels, local(): pl.pallas_call(functools.partial(far_kernel, total, count // 2, spot), ou...  2.03 us
    pallas_call x1, Pallas kernels, local(): pl.pallas_call(functools.partial(near_kernel, total, spot), out_shape=jax...  1.99 us
    ppermute x1, waiting for transfers between devices, local(): halo = lax.ppermute(edge, ('tm', 'chan'), to_previous(order, groups))  1.86 us
    ppermute x1, waiting for transfers between devices, local(): theirs = lax.ppermute(ours, 'tm', [(t, t ^ 1) for t in range(count)])  1.35 us
    ppermute x1, starting transfers between devices, local(): halo = lax.ppermute(edge, ('tm', 'chan'), to_previous(order, groups))  1.34 us
  transfers between devices with their start and end apart: 2, of which 2 were waited for; matrix products, arithmetic and copies ran while one was open for 0% of the time, Pallas kernels for 3%

profile of v4, /device:TPU:1, one launch (start us, length us, event | category | flops | bytes accessed | tf_op | source)
XLA Modules:
  0.0 57.2 jit_solution(3915157510353673583)
XLA Ops:
  0.0 32.0 %all_to_all.17 = f32[512,2,128]{2,1,0:T(2,128)S(1)} all-to-all(f32[512,2,128]{2,1,0:T(2,128)} %bitcast.23), channel_id=1, replica_groups={{0,2,16,18,32,34,48,50,52,54,36,38,20,22,24,26,40,42,56,58,60,62,44,46,..., dimensions={0} | all-to-all | bytes 1048576 | tf_op jit(solution)/shard_map/all_to_all | solution.py:116
  32.1 1.3 %collective-permute-start = (f32[128,2,2,128]{3,2,1,0:T(2,128)S(1)}, f32[128,2,2,128]{3,2,1,0:T(2,128)S(1)}, u32[]{:S(2)}, u32[]{:S(2)}) collective-permute-start(f32[128,2,2,128]{3,2,1,0:T(2,128)S(1)} %slice.4), channel_id=1, source_target_pairs={{0,195},{2,0},{16,2},{18,16},{32,18},{34,32},{48,34},{50,48},{52,5... | collective-permute-start | bytes 786440 | tf_op jit(solution)/shard_map/ppermute | solution.py:118
  33.4 0.0 copy-start
  33.4 0.7 %copy-done = s32[512]{0:T(512)S(1)} copy-done((s32[512]{0:T(512)S(1)}, s32[512]{0:T(512)}, u32[]{:S(2)}) %copy-start) | copy-done | bytes 2072
  34.1 2.0 %shard_map.28.near_ref = f32[8,128]{1,0:T(8,128)S(1)} custom-call(s32[512]{0:T(512)S(1)} %copy-done, f32[1024,128]{1,0:T(8,128)S(1)} %bitcast.18), custom_call_target="tpu_custom_call" | custom-call | flops 20000000 | bytes 600000 | tf_op jit(solution)/shard_map/pallas_call | solution.py:125
  36.1 1.9 %collective-permute-done = f32[128,2,2,128]{3,2,1,0:T(2,128)S(1)} collective-permute-done((f32[128,2,2,128]{3,2,1,0:T(2,128)S(1)}, f32[128,2,2,128]{3,2,1,0:T(2,128)S(1)}, u32[]{:S(2)}, u32[]{:S(2)}) %collective-permute-start) | collective-permute-done | bytes 262176 | tf_op jit(solution)/shard_map/ppermute | solution.py:118
  37.9 2.0 %shard_map.29 = f32[256,128]{1,0:T(8,128)S(1)} custom-call(s32[512]{0:T(512)S(1)} %copy-done, s32[1]{0:T(128)} %bitcast.more_ref, f32[1024,128]{1,0:T(8,128)S(1)} %bitcast.19, f32[512,128]{1,0:T(8,128)S(1)} %bitcast.21, f32[8,128]{1,0:T(8,128)S(1)} %shard_map.28.near_ref), custom_call_target="tpu_custom_call" | custom-call | flops 20000000 | bytes 600000 | tf_op jit(solution)/shard_map/pallas_call | solution.py:134
  40.0 15.1 %all_to_all.18 = f32[64,4,128]{2,1,0:T(4,128)S(1)} all-to-all(f32[64,4,128]{2,1,0:T(4,128)S(1)} %bitcast.20), channel_id=1, replica_groups={{0,16,32,48,52,36,20,24,40,56,60,44,28,12,8,4,68,72,76,92,108,124,120,1..., dimensions={0} | all-to-all | bytes 262144 | tf_op jit(solution)/shard_map/all_to_all | solution.py:144
  55.1 0.0 collective-permute-start.1
  55.1 1.3 %collective-permute-done.1 = f32[256,128]{1,0:T(8,128)S(1)} collective-permute-done((f32[256,128]{1,0:T(8,128)S(1)}, f32[256,128]{1,0:T(8,128)S(1)}, u32[]{:S(2)}, u32[]{:S(2)}) %collective-permute-start.1) | collective-permute-done | bytes 131104 | tf_op jit(solution)/shard_map/ppermute | solution.py:145
  56.5 0.8 %pad_maximum_fusion = f32[64,2,4,128]{3,2,1,0:T(4,128)} fusion(f32[64,1,4,128]{3,2,1,0:T(4,128)S(1)} %get-tuple-element.6, f32[64,1,4,128]{3,2,1,0:T(4,128)S(1)} %get-tuple-element.5), kind=kLoop, calls=%fused_computation | loop fusion | flops 65536 | bytes 524288 | tf_op jit(solution)/shard_map/concatenate | solution.py:150
  (2 shorter events, 0.1 us)
Async XLA Ops:
  32.1 5.9 %collective-permute-start = (f32[128,2,2,128]{3,2,1,0:T(2,128)S(1)}, f32[128,2,2,128]{3,2,1,0:T(2,128)S(1)}, u32[]{:S(2)}, u32[]{:S(2)}) collective-permute-start(f32[128,2,2,128]{3,2,1,0:T(2,128)S(1)} %slice.4), channel_id=1, source_target_pairs={{0,195},{2,0},{16,2},{18,16},{32,18},{34,32},{48,34},{50,48},{52,5... | collective-permute-start | bytes 786440 | tf_op jit(solution)/shard_map/ppermute | solution.py:118
  33.4 0.7 %copy-start = (s32[512]{0:T(512)S(1)}, s32[512]{0:T(512)}, u32[]{:S(2)}) copy-start(s32[512]{0:T(512)} %offs_ref.3) | copy-start | bytes 6148
  55.1 1.3 %collective-permute-start.1 = (f32[256,128]{1,0:T(8,128)S(1)}, f32[256,128]{1,0:T(8,128)S(1)}, u32[]{:S(2)}, u32[]{:S(2)}) collective-permute-start(f32[256,128]{1,0:T(8,128)S(1)} %bitcast.22), channel_id=1, source_target_pairs={{0,2},{2,0},{4,6},{6,4},{8,10},{10,8},{12,14},{14,12},{16,18},{18,... | collective-permute-start | bytes 393224 | tf_op jit(solution)/shard_map/ppermute | solution.py:145

commit v5 on v4

--- a/solution.py
+++ b/solution.py
@@ -9,6 +9,12 @@
 
 LANES = 128
 VMEM_LIMIT = 6 * 2**20
+CHIPS = (
+    6, 10, 14, 13, 12, 8, 9, 5, 21, 22, 23, 7, 3, 2, 1, 0,
+    4, 20, 16, 32, 36, 52, 48, 49, 53, 57, 58, 59, 43, 39, 38, 42,
+    46, 45, 44, 28, 24, 40, 56, 60, 61, 62, 63, 47, 31, 15, 11, 27,
+    26, 30, 29, 25, 41, 37, 33, 17, 18, 19, 35, 34, 50, 51, 55, 54,
+)
 
 
 def sublanes():
@@ -52,8 +58,11 @@
     return jnp.maximum(peak, pltpu.roll(peak, 4, axis=0))
 
 
-def near_kernel(total, spot, offs_ref, main_ref, out_ref, a_ref, b_ref):
+def near_kernel(total, spot, table_ref, main_ref, out_ref, offs_ref, a_ref, b_ref, sem):
     half = total // 4
+    copy = pltpu.make_async_copy(table_ref, offs_ref, sem)
+    copy.start()
+    copy.wait()
 
     def get(t, r):
         one = main_ref[pl.ds(spot[t] * 8 + r, 4, stride=2), :]
@@ -84,17 +93,8 @@
 
 
 def walk(count):
-    side, cores = 4, 2
-    plane = [(x, 0) for x in range(side)]
-    for y in range(1, side):
-        xs = range(1, side)
-        plane += [(x, y) for x in (xs[::-1] if y % 2 else xs)]
-    plane += [(0, y) for y in range(side - 1, 0, -1)]
-    order = []
-    for z in range(count // (side * side * cores)):
-        for x, y in plane if z % 2 == 0 else plane[::-1]:
-            order += [((z * side + x) * side + y) * cores + core for core in range(cores)]
-    return order
+    assert count == 2 * len(CHIPS)
+    return [2 * chip + core for chip in CHIPS for core in range(2)]
 
 
 def to_previous(order, groups):
@@ -122,12 +122,12 @@
     scratch = [pltpu.VMEM((total // 2, 8, LANES), jnp.float32)] * 2
     params = pltpu.CompilerParams(vmem_limit_bytes=VMEM_LIMIT)
     cost = pl.CostEstimate(flops=20_000_000, bytes_accessed=600_000, transcendentals=0)
-    near = pl.pallas_call(
+    near, table = pl.pallas_call(
         functools.partial(near_kernel, total, spot),
-        out_shape=jax.ShapeDtypeStruct((8, LANES), jnp.float32),
-        in_specs=[smem, vmem],
-        out_specs=vmem,
-        scratch_shapes=scratch,
+        out_shape=(jax.ShapeDtypeStruct((8, LANES), jnp.float32), pltpu.SMEM(offsets.shape, jnp.int32)),
+        in_specs=[pl.BlockSpec(memory_space=pl.ANY), vmem],
+        out_specs=(vmem, smem),
+        scratch_shapes=scratch + [pltpu.SemaphoreType.DMA],
         compiler_params=params,
         cost_estimate=cost,
     )(offsets, main)
@@ -139,7 +139,7 @@
         scratch_shapes=scratch,
         compiler_params=params,
         cost_estimate=cost,
-    )(offsets, more, main, halo.reshape(-1, LANES), near)
+    )(table, more, main, halo.reshape(-1, LANES), near)
     cores = [order[core::2] for core in range(2)]
     ours = lax.all_to_all(best, "tm", 0, 0, axis_index_groups=cores, tiled=True)
     theirs = lax.ppermute(ours, "tm", [(t, t ^ 1) for t in range(count)])

time: 57.5 us -> 54.3 us (0.944)
  blocking collectives: 47.1 us -> 44.4 us
  starting transfers between devices: 1.34 us -> 0.46 us
  waiting for transfers between devices: 3.2 us -> 3.96 us
    all_to_all x1, blocking collectives: 32 us -> 30.4 us  [local(): lax.all_to_all(tiles, 'tm', 0, 0, axis_index_groups=[order], tiled=True)]
    all_to_all x1, blocking collectives: 15.1 us -> 14 us  [local(): ours = lax.all_to_all(best, 'tm', 0, 0, axis_index_groups=cores, tiled=True)]
    ppermute x1, starting transfers between devices: 1.34 us -> 0.45 us  [local(): halo = lax.ppermute(edge, ('tm', 'chan'), to_previous(order, groups))]
    ppermute x1, waiting for transfers between devices: 1.86 us -> 2.61 us  [local(): halo = lax.ppermute(edge, ('tm', 'chan'), to_previous(order, groups))]
  transfers between devices with their start and end apart: 2 -> 2, of which waited for: 2 -> 2; matrix products, arithmetic and copies ran while one was open for 0% -> 0% of each run, Pallas kernels for 3% -> 4%
where the time goes in v5:
time: 54.3 us; the launch traced here: 54.1 us
  blocking collectives  44.4 us (82%)
  waiting for transfers between devices  3.96 us (7%)
  Pallas kernels  3.73 us (7%)
  other arithmetic  0.81 us (1%)
  local copies, waits for them, and re-layouts  0.73 us (1%)
    all_to_all x1, blocking collectives, local(): lax.all_to_all(tiles, 'tm', 0, 0, axis_index_groups=[order], tiled=True)  30.4 us
    all_to_all x1, blocking collectives, local(): ours = lax.all_to_all(best, 'tm', 0, 0, axis_index_groups=cores, tiled=True)  14 us
    ppermute x1, waiting for transfers between devices, local(): halo = lax.ppermute(edge, ('tm', 'chan'), to_previous(order, groups))  2.61 us
    pallas_call x1, Pallas kernels, local(): pl.pallas_call(functools.partial(near_kernel, total, spot), out_shape=(ja...  2.12 us
    pallas_call x1, Pallas kernels, local(): pl.pallas_call(functools.partial(far_kernel, total, count // 2, spot), ou...  1.61 us
    ppermute x1, waiting for transfers between devices, local(): theirs = lax.ppermute(ours, 'tm', [(t, t ^ 1) for t in range(count)])  1.35 us
  transfers between devices with their start and end apart: 2, of which 2 were waited for; matrix products, arithmetic and copies ran while one was open for 0% of the time, Pallas kernels for 4%

profile of v5, /device:TPU:1, one launch (start us, length us, event | category | flops | bytes accessed | tf_op | source)
XLA Modules:
  0.0 54.1 jit_solution(7785773335310367477)
XLA Ops:
  0.0 30.4 %all_to_all.17 = f32[512,2,128]{2,1,0:T(2,128)S(1)} all-to-all(f32[512,2,128]{2,1,0:T(2,128)} %bitcast.23), channel_id=1, replica_groups={{24,26,40,42,56,58,52,54,48,50,32,34,36,38,20,22,84,86,88,90,92,94,28,3..., dimensions={0} | all-to-all | bytes 1048576 | tf_op jit(solution)/shard_map/all_to_all | solution.py:116
  30.4 0.5 collective-permute-start
  30.9 0.0 copy-start
  30.9 0.7 %copy-done = s32[512]{0:T(512)S(1)} copy-done((s32[512]{0:T(512)S(1)}, s32[512]{0:T(512)}, u32[]{:S(2)}) %copy-start) | copy-done | bytes 2072
  31.6 2.1 %shard_map.28 = (f32[8,128]{1,0:T(8,128)S(1)}, s32[512]{0:T(512)S(4)}) custom-call(s32[512]{0:T(512)S(1)} %copy-done, f32[1024,128]{1,0:T(8,128)S(1)} %bitcast.18), custom_call_target="tpu_custom_call" | custom-call | flops 20000000 | bytes 600000 | tf_op jit(solution)/shard_map/pallas_call | solution.py:125
  33.7 2.6 %collective-permute-done = f32[128,2,2,128]{3,2,1,0:T(2,128)S(1)} collective-permute-done((f32[128,2,2,128]{3,2,1,0:T(2,128)S(1)}, f32[128,2,2,128]{3,2,1,0:T(2,128)S(1)}, u32[]{:S(2)}, u32[]{:S(2)}) %collective-permute-start) | collective-permute-done | bytes 262176 | tf_op jit(solution)/shard_map/ppermute | solution.py:118
  36.3 1.6 %shard_map.29 = f32[256,128]{1,0:T(8,128)S(1)} custom-call(s32[512]{0:T(512)S(4)} %get-tuple-element.7.offs_ref, s32[1]{0:T(128)} %bitcast.3.more_ref, f32[1024,128]{1,0:T(8,128)S(1)} %bitcast.19, f32[512,128]{1,0:T(8,128)S(1)} %bitcast.21, f32[8,128]{1,0:T(8,128)S(1)} %get-tuple-element.8.near_ref), custom_call_target="tpu_custom_call" | custom-call | flops 20000000 | bytes 600000 | tf_op jit(solution)/shard_map/pallas_call | solution.py:134
  37.9 14.0 %all_to_all.18 = f32[64,4,128]{2,1,0:T(4,128)S(1)} all-to-all(f32[64,4,128]{2,1,0:T(4,128)S(1)} %bitcast.20), channel_id=1, replica_groups={{24,40,56,52,48,32,36,20,84,88,92,28,12,8,4,0,16,80,64,128,144,208,192,..., dimensions={0} | all-to-all | bytes 262144 | tf_op jit(solution)/shard_map/all_to_all | solution.py:144
  51.9 0.0 collective-permute-start.1
  51.9 1.3 %collective-permute-done.1 = f32[256,128]{1,0:T(8,128)S(1)} collective-permute-done((f32[256,128]{1,0:T(8,128)S(1)}, f32[256,128]{1,0:T(8,128)S(1)}, u32[]{:S(2)}, u32[]{:S(2)}) %collective-permute-start.1) | collective-permute-done | bytes 131104 | tf_op jit(solution)/shard_map/ppermute | solution.py:145
  53.3 0.8 %pad_maximum_fusion = f32[64,2,4,128]{3,2,1,0:T(4,128)} fusion(f32[64,1,4,128]{3,2,1,0:T(4,128)S(1)} %get-tuple-element.10, f32[64,1,4,128]{3,2,1,0:T(4,128)S(1)} %get-tuple-element.9), kind=kLoop, calls=%fused_computation | loop fusion | flops 65536 | bytes 524288 | tf_op jit(solution)/shard_map/concatenate | solution.py:150
  (2 shorter events, 0.1 us)
Async XLA Ops:
  30.4 5.9 %collective-permute-start = (f32[128,2,2,128]{3,2,1,0:T(2,128)S(1)}, f32[128,2,2,128]{3,2,1,0:T(2,128)S(1)}, u32[]{:S(2)}, u32[]{:S(2)}) collective-permute-start(f32[128,2,2,128]{3,2,1,0:T(2,128)S(1)} %slice.4), channel_id=1, source_target_pairs={{24,219},{26,24},{40,26},{42,40},{56,42},{58,56},{52,58},{54,52},{... | collective-permute-start | bytes 786440 | tf_op jit(solution)/shard_map/ppermute | solution.py:118
  30.9 0.7 %copy-start = (s32[512]{0:T(512)S(1)}, s32[512]{0:T(512)}, u32[]{:S(2)}) copy-start(s32[512]{0:T(512)} %table_ref.1) | copy-start | bytes 6148
  51.9 1.3 %collective-permute-start.1 = (f32[256,128]{1,0:T(8,128)S(1)}, f32[256,128]{1,0:T(8,128)S(1)}, u32[]{:S(2)}, u32[]{:S(2)}) collective-permute-start(f32[256,128]{1,0:T(8,128)S(1)} %bitcast.22), channel_id=1, source_target_pairs={{0,2},{2,0},{4,6},{6,4},{8,10},{10,8},{12,14},{14,12},{16,18},{18,... | collective-permute-start | bytes 393224 | tf_op jit(solution)/shard_map/ppermute | solution.py:145

commit v6 on v5

--- a/solution.py
+++ b/solution.py
@@ -10,10 +10,10 @@
 LANES = 128
 VMEM_LIMIT = 6 * 2**20
 CHIPS = (
-    6, 10, 14, 13, 12, 8, 9, 5, 21, 22, 23, 7, 3, 2, 1, 0,
-    4, 20, 16, 32, 36, 52, 48, 49, 53, 57, 58, 59, 43, 39, 38, 42,
-    46, 45, 44, 28, 24, 40, 56, 60, 61, 62, 63, 47, 31, 15, 11, 27,
-    26, 30, 29, 25, 41, 37, 33, 17, 18, 19, 35, 34, 50, 51, 55, 54,
+    10, 26, 25, 24, 28, 12, 8, 4, 0, 16, 20, 21, 22, 23, 27, 31,
+    30, 14, 15, 11, 7, 3, 19, 18, 17, 1, 2, 6, 5, 9, 13, 29,
+    45, 46, 47, 63, 59, 55, 51, 50, 54, 53, 57, 56, 52, 48, 49, 33,
+    32, 36, 37, 38, 34, 35, 39, 43, 42, 41, 40, 44, 60, 61, 62, 58,
 )
 
 
@@ -29,10 +29,12 @@
 
 def tree(offs_ref, get, total, a_ref, b_ref):
     half = total // 2
+    step = jnp.full((8, LANES), offs_ref[2], jnp.int32) > 0
     for q in range(half // 2):
         lower, upper = get(q, 0), get(q, 1)
-        for d in range(2):
-            b_ref[2 * q + d] = lower + moved(upper, offs_ref[2 + d])
+        by_one = moved(upper, 1)
+        b_ref[2 * q] = lower + jnp.where(step, by_one, upper)
+        b_ref[2 * q + 1] = lower + by_one
     src, dst = b_ref, a_ref
     length = 2
     while length < half:
@@ -81,8 +83,8 @@
         one, two = spot[t], spot[t + half]
         head_one = main_ref[pl.ds(one * 8 + r + 4, 2, stride=2), :]
         head_two = main_ref[pl.ds(two * 8 + r + 4, 2, stride=2), :]
-        tail_one = halo_ref[pl.ds(one * 4 + r, 2, stride=2), :]
-        tail_two = halo_ref[pl.ds(two * 4 + r, 2, stride=2), :]
+        tail_one = halo_ref[pl.ds(3 * half * r + one, 2, stride=half), :]
+        tail_two = halo_ref[pl.ds(3 * half * r + two, 2, stride=half), :]
         both = jnp.concatenate([head_one, tail_one, head_two, tail_two], axis=0)
         return jnp.where(keep, both, 0.0)
 
@@ -114,7 +116,10 @@
     more = jnp.reshape(more, (1,)).astype(jnp.int32)
     tiles = spectrum.reshape(rows, span // LANES, LANES).transpose(1, 0, 2)
     main = lax.all_to_all(tiles, "tm", 0, 0, axis_index_groups=[order], tiled=True)
-    edge = main.reshape(count, cols, rows, LANES)[:, : cols // 2]
+    early = count // 2
+    assert max(order[:early]) < early
+    window = main.reshape(count, cols, rows, LANES)
+    edge = jnp.concatenate([window[:, 0], window[early:, 1]], axis=0)
     halo = lax.ppermute(edge, ("tm", "chan"), to_previous(order, groups))
     main = main.reshape(-1, LANES)
     smem = pl.BlockSpec(memory_space=pltpu.SMEM)
@@ -139,7 +144,7 @@
         scratch_shapes=scratch,
         compiler_params=params,
         cost_estimate=cost,
-    )(table, more, main, halo.reshape(-1, LANES), near)
+    )(table, more, main, halo.transpose(1, 0, 2).reshape(-1, LANES), near)
     cores = [order[core::2] for core in range(2)]
     ours = lax.all_to_all(best, "tm", 0, 0, axis_index_groups=cores, tiled=True)
     theirs = lax.ppermute(ours, "tm", [(t, t ^ 1) for t in range(count)])

time: 54.3 us -> 52.9 us (0.974)
  blocking collectives: 44.4 us -> 43.3 us
  waiting for transfers between devices: 3.96 us -> 2.96 us
  starting transfers between devices: 0.46 us -> 1.08 us
    all_to_all x1, blocking collectives: 30.4 us -> 29.7 us  [local(): lax.all_to_all(tiles, 'tm', 0, 0, axis_index_groups=[order], tiled=True)]
    ppermute x1, waiting for transfers between devices: 2.61 us -> 1.97 us  [local(): halo = lax.ppermute(edge, ('tm', 'chan'), to_previous(order, groups))]
    ppermute x1, starting transfers between devices: 0.01 us -> 0.61 us  [local(): theirs = lax.ppermute(ours, 'tm', [(t, t ^ 1) for t in range(count)])]
where the time goes in v6:
time: 52.9 us; the launch traced here: 52.7 us
  blocking collectives  43.3 us (82%)
  Pallas kernels  3.63 us (7%)
  waiting for transfers between devices  2.96 us (6%)
  starting transfers between devices  1.08 us (2%)
  local copies, waits for them, and re-layouts  0.88 us (2%)
  other arithmetic  0.82 us (2%)
    all_to_all x1, blocking collectives, local(): lax.all_to_all(tiles, 'tm', 0, 0, axis_index_groups=[order], tiled=True)  29.7 us
    all_to_all x1, blocking collectives, local(): ours = lax.all_to_all(best, 'tm', 0, 0, axis_index_groups=cores, tiled=True)  13.6 us
    pallas_call x1, Pallas kernels, local(): pl.pallas_call(functools.partial(near_kernel, total, spot), out_shape=(ja...  2.04 us
    ppermute x1, waiting for transfers between devices, local(): halo = lax.ppermute(edge, ('tm', 'chan'), to_previous(order, groups))  1.97 us
    pallas_call x1, Pallas kernels, local(): pl.pallas_call(functools.partial(far_kernel, total, count // 2, spot), ou...  1.59 us
  transfers between devices with their start and end apart: 2, of which 2 were waited for; matrix products, arithmetic and copies ran while one was open for 0% of the time, Pallas kernels for 4%

profile of v6, /device:TPU:1, one launch (start us, length us, event | category | flops | bytes accessed | tf_op | source)
XLA Modules:
  0.0 52.7 jit_solution(12536956374328294017)
XLA Ops:
  0.0 29.7 %all_to_all.17 = f32[512,2,128]{2,1,0:T(2,128)S(1)} all-to-all(f32[512,2,128]{2,1,0:T(2,128)} %bitcast.29), channel_id=1, replica_groups={{40,42,104,106,100,102,96,98,112,114,48,50,32,34,16,18,0,2,64,66,80,82,..., dimensions={0} | all-to-all | bytes 1048576 | tf_op jit(solution)/shard_map/all_to_all | solution.py:118
  29.7 0.1 slice.8
  29.8 0.1 slice.9
  29.9 0.5 collective-permute-start
  30.4 0.0 copy-start
  30.4 0.7 %copy-done = s32[512]{0:T(512)S(1)} copy-done((s32[512]{0:T(512)S(1)}, s32[512]{0:T(512)}, u32[]{:S(2)}) %copy-start) | copy-done | bytes 2072
  31.1 2.0 %shard_map.28 = (f32[8,128]{1,0:T(8,128)S(1)}, s32[512]{0:T(512)S(4)}) custom-call(s32[512]{0:T(512)S(1)} %copy-done, f32[1024,128]{1,0:T(8,128)S(1)} %bitcast.21), custom_call_target="tpu_custom_call" | custom-call | flops 20000000 | bytes 600000 | tf_op jit(solution)/shard_map/pallas_call | solution.py:130
  33.1 2.0 %collective-permute-done = f32[192,2,128]{2,0,1:T(8,128)S(1)} collective-permute-done((f32[192,2,128]{2,0,1:T(8,128)S(1)}, f32[192,2,128]{2,0,1:T(8,128)S(1)}, u32[]{:S(2)}, u32[]{:S(2)}) %collective-permute-start) | collective-permute-done | bytes 196640 | tf_op jit(solution)/shard_map/ppermute | solution.py:123
  35.1 1.6 %shard_map.29 = f32[256,128]{1,0:T(8,128)S(1)} custom-call(s32[512]{0:T(512)S(4)} %get-tuple-element.7.offs_ref, s32[1]{0:T(128)} %bitcast.3.more_ref, f32[1024,128]{1,0:T(8,128)S(1)} %bitcast.22, f32[384,128]{1,0:T(8,128)S(1)} %bitcast.24, f32[8,128]{1,0:T(8,128)S(1)} %get-tuple-element.8.near_ref), custom_call_target="tpu_custom_call" | custom-call | flops 20000000 | bytes 600000 | tf_op jit(solution)/shard_map/pallas_call | solution.py:139
  36.7 13.6 %all_to_all.18 = f32[64,4,128]{2,1,0:T(4,128)S(1)} all-to-all(f32[64,4,128]{2,1,0:T(4,128)S(1)} %bitcast.23), channel_id=1, replica_groups={{40,104,100,96,112,48,32,16,0,64,80,84,88,92,108,124,120,56,60,44,28,12..., dimensions={0} | all-to-all | bytes 262144 | tf_op jit(solution)/shard_map/all_to_all | solution.py:149
  50.3 0.6 %collective-permute-start.1 = (f32[256,128]{1,0:T(8,128)S(1)}, f32[256,128]{1,0:T(8,128)S(1)}, u32[]{:S(2)}, u32[]{:S(2)}) collective-permute-start(f32[256,128]{1,0:T(8,128)S(1)} %bitcast.27), channel_id=1, source_target_pairs={{0,2},{2,0},{4,6},{6,4},{8,10},{10,8},{12,14},{14,12},{16,18},{18,... | collective-permute-start | bytes 393224 | tf_op jit(solution)/shard_map/ppermute | solution.py:150
  50.9 1.0 %collective-permute-done.1 = f32[256,128]{1,0:T(8,128)S(1)} collective-permute-done((f32[256,128]{1,0:T(8,128)S(1)}, f32[256,128]{1,0:T(8,128)S(1)}, u32[]{:S(2)}, u32[]{:S(2)}) %collective-permute-start.1) | collective-permute-done | bytes 131104 | tf_op jit(solution)/shard_map/ppermute | solution.py:150
  51.9 0.8 %pad_maximum_fusion = f32[64,2,4,128]{3,2,1,0:T(4,128)} fusion(f32[64,1,4,128]{3,2,1,0:T(4,128)S(1)} %get-tuple-element.10, f32[64,1,4,128]{3,2,1,0:T(4,128)S(1)} %get-tuple-element.9), kind=kLoop, calls=%fused_computation | loop fusion | flops 65536 | bytes 524288 | tf_op jit(solution)/shard_map/concatenate | solution.py:155
  (3 shorter events, 0.1 us)
Async XLA Ops:
  29.9 5.2 %collective-permute-start = (f32[192,2,128]{2,0,1:T(8,128)S(1)}, f32[192,2,128]{2,0,1:T(8,128)S(1)}, u32[]{:S(2)}, u32[]{:S(2)}) collective-permute-start(f32[192,2,128]{2,0,1:T(8,128)S(1)} %pad_maximum_fusion.1), channel_id=1, source_target_pairs={{40,235},{42,40},{104,42},{106,104},{100,106},{102,100},{96,102},{... | collective-permute-start | bytes 589832 | tf_op jit(solution)/shard_map/ppermute | solution.py:123
  30.4 0.7 %copy-start = (s32[512]{0:T(512)S(1)}, s32[512]{0:T(512)}, u32[]{:S(2)}) copy-start(s32[512]{0:T(512)} %table_ref.1) | copy-start | bytes 6148
  50.3 1.6 %collective-permute-start.1 = (f32[256,128]{1,0:T(8,128)S(1)}, f32[256,128]{1,0:T(8,128)S(1)}, u32[]{:S(2)}, u32[]{:S(2)}) collective-permute-start(f32[256,128]{1,0:T(8,128)S(1)} %bitcast.27), channel_id=1, source_target_pairs={{0,2},{2,0},{4,6},{6,4},{8,10},{10,8},{12,14},{14,12},{16,18},{18,... | collective-permute-start | bytes 393224 | tf_op jit(solution)/shard_map/ppermute | solution.py:150

commit v7 on v6

--- a/solution.py
+++ b/solution.py
@@ -10,10 +10,10 @@
 LANES = 128
 VMEM_LIMIT = 6 * 2**20
 CHIPS = (
-    10, 26, 25, 24, 28, 12, 8, 4, 0, 16, 20, 21, 22, 23, 27, 31,
-    30, 14, 15, 11, 7, 3, 19, 18, 17, 1, 2, 6, 5, 9, 13, 29,
-    45, 46, 47, 63, 59, 55, 51, 50, 54, 53, 57, 56, 52, 48, 49, 33,
-    32, 36, 37, 38, 34, 35, 39, 43, 42, 41, 40, 44, 60, 61, 62, 58,
+    10, 14, 15, 31, 27, 11, 7, 6, 5, 9, 13, 12, 28, 29, 30, 26,
+    25, 24, 8, 4, 20, 16, 0, 1, 2, 3, 19, 23, 22, 18, 17, 21,
+    37, 38, 39, 35, 51, 55, 59, 43, 42, 41, 57, 61, 62, 63, 47, 46,
+    45, 44, 60, 56, 40, 36, 32, 48, 52, 53, 49, 33, 34, 50, 54, 58,
 )
 
 

time: 52.9 us -> 53.1 us (level)
  no operation moved by 1% of the time
where the time goes in v7:
time: 53.1 us; the launch traced here: 52.9 us
  blocking collectives  43.7 us (82%)
  Pallas kernels  3.63 us (7%)
  waiting for transfers between devices  2.8 us (5%)
  starting transfers between devices  1.03 us (2%)
  local copies, waits for them, and re-layouts  0.88 us (2%)
  other arithmetic  0.82 us (2%)
    all_to_all x1, blocking collectives, local(): lax.all_to_all(tiles, 'tm', 0, 0, axis_index_groups=[order], tiled=True)  29.6 us
    all_to_all x1, blocking collectives, local(): ours = lax.all_to_all(best, 'tm', 0, 0, axis_index_groups=cores, tiled=True)  14.1 us
    pallas_call x1, Pallas kernels, local(): pl.pallas_call(functools.partial(near_kernel, total, spot), out_shape=(ja...  2.04 us
    ppermute x1, waiting for transfers between devices, local(): halo = lax.ppermute(edge, ('tm', 'chan'), to_previous(order, groups))  1.81 us
    pallas_call x1, Pallas kernels, local(): pl.pallas_call(functools.partial(far_kernel, total, count // 2, spot), ou...  1.59 us
  transfers between devices with their start and end apart: 2, of which 2 were waited for; matrix products, arithmetic and copies ran while one was open for 0% of the time, Pallas kernels for 4%

profile of v7, /device:TPU:1, one launch (start us, length us, event | category | flops | bytes accessed | tf_op | source)
XLA Modules:
  0.0 52.9 jit_solution(3906053850244998093)
XLA Ops:
  0.0 29.6 %all_to_all.17 = f32[512,2,128]{2,1,0:T(2,128)S(1)} all-to-all(f32[512,2,128]{2,1,0:T(2,128)} %bitcast.29), channel_id=1, replica_groups={{40,42,56,58,60,62,124,126,108,110,44,46,28,30,24,26,20,22,36,38,52,54,..., dimensions={0} | all-to-all | bytes 1048576 | tf_op jit(solution)/shard_map/all_to_all | solution.py:118
  29.6 0.1 slice.8
  29.7 0.1 slice.9
  29.8 0.6 %collective-permute-start = (f32[192,2,128]{2,0,1:T(8,128)S(1)}, f32[192,2,128]{2,0,1:T(8,128)S(1)}, u32[]{:S(2)}, u32[]{:S(2)}) collective-permute-start(f32[192,2,128]{2,0,1:T(8,128)S(1)} %pad_maximum_fusion.1), channel_id=1, source_target_pairs={{40,235},{42,40},{56,42},{58,56},{60,58},{62,60},{124,62},{126,124... | collective-permute-start | bytes 589832 | tf_op jit(solution)/shard_map/ppermute | solution.py:123
  30.4 0.0 copy-start
  30.4 0.7 %copy-done = s32[512]{0:T(512)S(1)} copy-done((s32[512]{0:T(512)S(1)}, s32[512]{0:T(512)}, u32[]{:S(2)}) %copy-start) | copy-done | bytes 2072
  31.1 2.0 %shard_map.28 = (f32[8,128]{1,0:T(8,128)S(1)}, s32[512]{0:T(512)S(4)}) custom-call(s32[512]{0:T(512)S(1)} %copy-done, f32[1024,128]{1,0:T(8,128)S(1)} %bitcast.21), custom_call_target="tpu_custom_call" | custom-call | flops 20000000 | bytes 600000 | tf_op jit(solution)/shard_map/pallas_call | solution.py:130
  33.2 1.8 %collective-permute-done = f32[192,2,128]{2,0,1:T(8,128)S(1)} collective-permute-done((f32[192,2,128]{2,0,1:T(8,128)S(1)}, f32[192,2,128]{2,0,1:T(8,128)S(1)}, u32[]{:S(2)}, u32[]{:S(2)}) %collective-permute-start) | collective-permute-done | bytes 196640 | tf_op jit(solution)/shard_map/ppermute | solution.py:123
  35.0 1.6 %shard_map.29 = f32[256,128]{1,0:T(8,128)S(1)} custom-call(s32[512]{0:T(512)S(4)} %get-tuple-element.7.offs_ref, s32[1]{0:T(128)} %bitcast.3.more_ref, f32[1024,128]{1,0:T(8,128)S(1)} %bitcast.22, f32[384,128]{1,0:T(8,128)S(1)} %bitcast.24, f32[8,128]{1,0:T(8,128)S(1)} %get-tuple-element.8.near_ref), custom_call_target="tpu_custom_call" | custom-call | flops 20000000 | bytes 600000 | tf_op jit(solution)/shard_map/pallas_call | solution.py:139
  36.6 14.1 %all_to_all.18 = f32[64,4,128]{2,1,0:T(4,128)S(1)} all-to-all(f32[64,4,128]{2,1,0:T(4,128)S(1)} %bitcast.23), channel_id=1, replica_groups={{40,56,60,124,108,44,28,24,20,36,52,48,112,116,120,104,100,96,32,16,80,..., dimensions={0} | all-to-all | bytes 262144 | tf_op jit(solution)/shard_map/all_to_all | solution.py:149
  50.7 0.4 collective-permute-start.1
  51.1 1.0 %collective-permute-done.1 = f32[256,128]{1,0:T(8,128)S(1)} collective-permute-done((f32[256,128]{1,0:T(8,128)S(1)}, f32[256,128]{1,0:T(8,128)S(1)}, u32[]{:S(2)}, u32[]{:S(2)}) %collective-permute-start.1) | collective-permute-done | bytes 131104 | tf_op jit(solution)/shard_map/ppermute | solution.py:150
  52.1 0.8 %pad_maximum_fusion = f32[64,2,4,128]{3,2,1,0:T(4,128)} fusion(f32[64,1,4,128]{3,2,1,0:T(4,128)S(1)} %get-tuple-element.10, f32[64,1,4,128]{3,2,1,0:T(4,128)S(1)} %get-tuple-element.9), kind=kLoop, calls=%fused_computation | loop fusion | flops 65536 | bytes 524288 | tf_op jit(solution)/shard_map/concatenate | solution.py:155
  (3 shorter events, 0.1 us)
Async XLA Ops:
  29.8 5.2 %collective-permute-start = (f32[192,2,128]{2,0,1:T(8,128)S(1)}, f32[192,2,128]{2,0,1:T(8,128)S(1)}, u32[]{:S(2)}, u32[]{:S(2)}) collective-permute-start(f32[192,2,128]{2,0,1:T(8,128)S(1)} %pad_maximum_fusion.1), channel_id=1, source_target_pairs={{40,235},{42,40},{56,42},{58,56},{60,58},{62,60},{124,62},{126,124... | collective-permute-start | bytes 589832 | tf_op jit(solution)/shard_map/ppermute | solution.py:123
  30.4 0.7 %copy-start = (s32[512]{0:T(512)S(1)}, s32[512]{0:T(512)}, u32[]{:S(2)}) copy-start(s32[512]{0:T(512)} %table_ref.1) | copy-start | bytes 6148
  50.7 1.4 %collective-permute-start.1 = (f32[256,128]{1,0:T(8,128)S(1)}, f32[256,128]{1,0:T(8,128)S(1)}, u32[]{:S(2)}, u32[]{:S(2)}) collective-permute-start(f32[256,128]{1,0:T(8,128)S(1)} %bitcast.27), channel_id=1, source_target_pairs={{0,2},{2,0},{4,6},{6,4},{8,10},{10,8},{12,14},{14,12},{16,18},{18,... | collective-permute-start | bytes 393224 | tf_op jit(solution)/shard_map/ppermute | solution.py:150

commit v8 on v7

--- a/solution.py
+++ b/solution.py
@@ -15,6 +15,7 @@
     37, 38, 39, 35, 51, 55, 59, 43, 42, 41, 57, 61, 62, 63, 47, 46,
     45, 44, 60, 56, 40, 36, 32, 48, 52, 53, 49, 33, 34, 50, 54, 58,
 )
+LEAD = 40
 
 
 def sublanes():
@@ -145,14 +146,16 @@
         compiler_params=params,
         cost_estimate=cost,
     )(table, more, main, halo.transpose(1, 0, 2).reshape(-1, LANES), near)
-    cores = [order[core::2] for core in range(2)]
+    turned = order[2 * LEAD :] + order[: 2 * LEAD]
+    cores = [turned[core::2] for core in range(2)]
     ours = lax.all_to_all(best, "tm", 0, 0, axis_index_groups=cores, tiled=True)
     theirs = lax.ppermute(ours, "tm", [(t, t ^ 1) for t in range(count)])
     pair = [part.reshape(count // 2, 1, cols, LANES) for part in (ours, theirs)]
     second = lax.axis_index("tm") % 2 == 1
     first_core = jnp.where(second, pair[1], pair[0])
     second_core = jnp.where(second, pair[0], pair[1])
-    return jnp.concatenate([first_core, second_core], axis=1).reshape(span)
+    both = jnp.concatenate([first_core, second_core], axis=1)
+    return jnp.roll(both, LEAD, axis=0).reshape(span)
 
 
 def solution(mesh):

time: 53.1 us -> 52.6 us (level)
  blocking collectives: 43.7 us -> 42.6 us
    all_to_all x1, blocking collectives: 14.1 us -> 13.1 us  [local(): ours = lax.all_to_all(best, 'tm', 0, 0, axis_index_groups=cores, tiled=True)]
where the time goes in v8:
time: 52.6 us; the launch traced here: 52.4 us
  blocking collectives  42.6 us (81%)
  Pallas kernels  3.63 us (7%)
  waiting for transfers between devices  2.8 us (5%)
  starting transfers between devices  1.52 us (3%)
  local copies, waits for them, and re-layouts  0.88 us (2%)
  other arithmetic  0.86 us (2%)
    all_to_all x1, blocking collectives, local(): lax.all_to_all(tiles, 'tm', 0, 0, axis_index_groups=[order], tiled=True)  29.6 us
    all_to_all x1, blocking collectives, local(): ours = lax.all_to_all(best, 'tm', 0, 0, axis_index_groups=cores, tiled=True)  13.1 us
    pallas_call x1, Pallas kernels, local(): pl.pallas_call(functools.partial(near_kernel, total, spot), out_shape=(ja...  2.04 us
    ppermute x1, waiting for transfers between devices, local(): halo = lax.ppermute(edge, ('tm', 'chan'), to_previous(order, groups))  1.81 us
    pallas_call x1, Pallas kernels, local(): pl.pallas_call(functools.partial(far_kernel, total, count // 2, spot), ou...  1.59 us
  transfers between devices with their start and end apart: 2, of which 2 were waited for; matrix products, arithmetic and copies ran while one was open for 0% of the time, Pallas kernels for 4%

profile of v8, /device:TPU:1, one launch (start us, length us, event | category | flops | bytes accessed | tf_op | source)
XLA Modules:
  0.0 52.4 jit_solution(6046834476773582934)
XLA Ops:
  0.0 29.6 %all_to_all.17 = f32[512,2,128]{2,1,0:T(2,128)S(1)} all-to-all(f32[512,2,128]{2,1,0:T(2,128)} %bitcast.29), channel_id=1, replica_groups={{40,42,56,58,60,62,124,126,108,110,44,46,28,30,24,26,20,22,36,38,52,54,..., dimensions={0} | all-to-all | bytes 1048576 | tf_op jit(solution)/shard_map/all_to_all | solution.py:119
  29.6 0.1 slice.18
  29.7 0.1 slice.19
  29.8 0.6 %collective-permute-start = (f32[192,2,128]{2,0,1:T(8,128)S(1)}, f32[192,2,128]{2,0,1:T(8,128)S(1)}, u32[]{:S(2)}, u32[]{:S(2)}) collective-permute-start(f32[192,2,128]{2,0,1:T(8,128)S(1)} %pad_maximum_fusion.1), channel_id=1, source_target_pairs={{40,235},{42,40},{56,42},{58,56},{60,58},{62,60},{124,62},{126,124... | collective-permute-start | bytes 589832 | tf_op jit(solution)/shard_map/ppermute | solution.py:124
  30.4 0.0 copy-start
  30.4 0.7 %copy-done = s32[512]{0:T(512)S(1)} copy-done((s32[512]{0:T(512)S(1)}, s32[512]{0:T(512)}, u32[]{:S(2)}) %copy-start) | copy-done | bytes 2072
  31.1 2.0 %shard_map.28 = (f32[8,128]{1,0:T(8,128)S(1)}, s32[512]{0:T(512)S(4)}) custom-call(s32[512]{0:T(512)S(1)} %copy-done, f32[1024,128]{1,0:T(8,128)S(1)} %bitcast.21), custom_call_target="tpu_custom_call" | custom-call | flops 20000000 | bytes 600000 | tf_op jit(solution)/shard_map/pallas_call | solution.py:131
  33.2 1.8 %collective-permute-done = f32[192,2,128]{2,0,1:T(8,128)S(1)} collective-permute-done((f32[192,2,128]{2,0,1:T(8,128)S(1)}, f32[192,2,128]{2,0,1:T(8,128)S(1)}, u32[]{:S(2)}, u32[]{:S(2)}) %collective-permute-start) | collective-permute-done | bytes 196640 | tf_op jit(solution)/shard_map/ppermute | solution.py:124
  35.0 1.6 %shard_map.29 = f32[256,128]{1,0:T(8,128)S(1)} custom-call(s32[512]{0:T(512)S(4)} %get-tuple-element.7.offs_ref, s32[1]{0:T(128)} %bitcast.3.more_ref, f32[1024,128]{1,0:T(8,128)S(1)} %bitcast.22, f32[384,128]{1,0:T(8,128)S(1)} %bitcast.24, f32[8,128]{1,0:T(8,128)S(1)} %get-tuple-element.8.near_ref), custom_call_target="tpu_custom_call" | custom-call | flops 20000000 | bytes 600000 | tf_op jit(solution)/shard_map/pallas_call | solution.py:140
  36.6 13.1 %all_to_all.18 = f32[64,4,128]{2,1,0:T(4,128)S(1)} all-to-all(f32[64,4,128]{2,1,0:T(4,128)S(1)} %bitcast.23), channel_id=1, replica_groups={{168,164,228,244,248,252,188,184,180,176,240,224,160,144,128,192,208,21..., dimensions={0} | all-to-all | bytes 262144 | tf_op jit(solution)/shard_map/all_to_all | solution.py:151
  49.6 0.9 %collective-permute-start.1 = (f32[256,128]{1,0:T(8,128)S(1)}, f32[256,128]{1,0:T(8,128)S(1)}, u32[]{:S(2)}, u32[]{:S(2)}) collective-permute-start(f32[256,128]{1,0:T(8,128)S(1)} %bitcast.27), channel_id=1, source_target_pairs={{0,2},{2,0},{4,6},{6,4},{8,10},{10,8},{12,14},{14,12},{16,18},{18,... | collective-permute-start | bytes 393224 | tf_op jit(solution)/shard_map/ppermute | solution.py:152
  50.5 1.0 %collective-permute-done.1 = f32[256,128]{1,0:T(8,128)S(1)} collective-permute-done((f32[256,128]{1,0:T(8,128)S(1)}, f32[256,128]{1,0:T(8,128)S(1)}, u32[]{:S(2)}, u32[]{:S(2)}) %collective-permute-start.1) | collective-permute-done | bytes 131104 | tf_op jit(solution)/shard_map/ppermute | solution.py:152
  51.6 0.8 %fusion = f32[64,2,4,128]{3,2,1,0:T(4,128)} fusion(f32[64,1,4,128]{3,2,1,0:T(4,128)S(1)} %get-tuple-element.10, f32[64,1,4,128]{3,2,1,0:T(4,128)S(1)} %get-tuple-element.9, f32[40,2,4,128]{3,2,1,0:T(4,128)S(1)} %fusion.1), kind=kLoop, calls=%fused_computation.1 | loop fusion | flops 131072 | bytes 688128 | tf_op jit(solution)/shard_map/jit(_roll_static)/concatenate | solution.py:158
  (4 shorter events, 0.1 us)
Async XLA Ops:
  29.8 5.2 %collective-permute-start = (f32[192,2,128]{2,0,1:T(8,128)S(1)}, f32[192,2,128]{2,0,1:T(8,128)S(1)}, u32[]{:S(2)}, u32[]{:S(2)}) collective-permute-start(f32[192,2,128]{2,0,1:T(8,128)S(1)} %pad_maximum_fusion.1), channel_id=1, source_target_pairs={{40,235},{42,40},{56,42},{58,56},{60,58},{62,60},{124,62},{126,124... | collective-permute-start | bytes 589832 | tf_op jit(solution)/shard_map/ppermute | solution.py:124
  30.4 0.7 %copy-start = (s32[512]{0:T(512)S(1)}, s32[512]{0:T(512)}, u32[]{:S(2)}) copy-start(s32[512]{0:T(512)} %table_ref.1) | copy-start | bytes 6148
  49.6 1.9 %collective-permute-start.1 = (f32[256,128]{1,0:T(8,128)S(1)}, f32[256,128]{1,0:T(8,128)S(1)}, u32[]{:S(2)}, u32[]{:S(2)}) collective-permute-start(f32[256,128]{1,0:T(8,128)S(1)} %bitcast.27), channel_id=1, source_target_pairs={{0,2},{2,0},{4,6},{6,4},{8,10},{10,8},{12,14},{14,12},{16,18},{18,... | collective-permute-start | bytes 393224 | tf_op jit(solution)/shard_map/ppermute | solution.py:152

commit v9 on v8

--- a/solution.py
+++ b/solution.py
@@ -10,12 +10,12 @@
 LANES = 128
 VMEM_LIMIT = 6 * 2**20
 CHIPS = (
-    10, 14, 15, 31, 27, 11, 7, 6, 5, 9, 13, 12, 28, 29, 30, 26,
-    25, 24, 8, 4, 20, 16, 0, 1, 2, 3, 19, 23, 22, 18, 17, 21,
-    37, 38, 39, 35, 51, 55, 59, 43, 42, 41, 57, 61, 62, 63, 47, 46,
-    45, 44, 60, 56, 40, 36, 32, 48, 52, 53, 49, 33, 34, 50, 54, 58,
+    10, 26, 25, 9, 13, 12, 8, 24, 28, 29, 30, 14, 15, 31, 27, 11,
+    7, 3, 19, 18, 17, 21, 5, 4, 20, 16, 0, 1, 2, 6, 22, 23,
+    39, 35, 34, 38, 54, 55, 51, 50, 49, 53, 52, 48, 32, 33, 37, 36,
+    40, 56, 60, 44, 45, 61, 57, 41, 42, 46, 47, 43, 59, 63, 62, 58,
 )
-LEAD = 40
+LEAD = 56
 
 
 def sublanes():

time: 52.6 us -> 52 us (0.989)
  starting transfers between devices: 1.52 us -> 0.47 us
    ppermute x1, starting transfers between devices: 0.89 us -> 0.01 us  [local(): theirs = lax.ppermute(ours, 'tm', [(t, t ^ 1) for t in range(count)])]
where the time goes in v9:
time: 52 us; the launch traced here: 51.8 us
  blocking collectives  42.5 us (82%)
  Pallas kernels  3.63 us (7%)
  waiting for transfers between devices  3.32 us (6%)
  local copies, waits for them, and re-layouts  0.88 us (2%)
  other arithmetic  0.88 us (2%)
    all_to_all x1, blocking collectives, local(): lax.all_to_all(tiles, 'tm', 0, 0, axis_index_groups=[order], tiled=True)  29.6 us
    all_to_all x1, blocking collectives, local(): ours = lax.all_to_all(best, 'tm', 0, 0, axis_index_groups=cores, tiled=True)  12.9 us
    pallas_call x1, Pallas kernels, local(): pl.pallas_call(functools.partial(near_kernel, total, spot), out_shape=(ja...  2.04 us
    ppermute x1, waiting for transfers between devices, local(): halo = lax.ppermute(edge, ('tm', 'chan'), to_previous(order, groups))  1.97 us
    pallas_call x1, Pallas kernels, local(): pl.pallas_call(functools.partial(far_kernel, total, count // 2, spot), ou...  1.59 us
    ppermute x1, waiting for transfers between devices, local(): theirs = lax.ppermute(ours, 'tm', [(t, t ^ 1) for t in range(count)])  1.35 us
  transfers between devices with their start and end apart: 2, of which 2 were waited for; matrix products, arithmetic and copies ran while one was open for 0% of the time, Pallas kernels for 4%

profile of v9, /device:TPU:1, one launch (start us, length us, event | category | flops | bytes accessed | tf_op | source)
XLA Modules:
  0.0 51.8 jit_solution(14726327278984784632)
XLA Ops:
  0.0 29.6 %all_to_all.17 = f32[512,2,128]{2,1,0:T(2,128)S(1)} all-to-all(f32[512,2,128]{2,1,0:T(2,128)} %bitcast.29), channel_id=1, replica_groups={{40,42,104,106,100,102,36,38,52,54,48,50,32,34,96,98,112,114,116,118,12..., dimensions={0} | all-to-all | bytes 1048576 | tf_op jit(solution)/shard_map/all_to_all | solution.py:119
  29.6 0.1 slice.18
  29.7 0.1 slice.19
  29.8 0.5 collective-permute-start
  30.3 0.0 copy-start
  30.3 0.7 %copy-done = s32[512]{0:T(512)S(1)} copy-done((s32[512]{0:T(512)S(1)}, s32[512]{0:T(512)}, u32[]{:S(2)}) %copy-start) | copy-done | bytes 2072
  31.0 2.0 %shard_map.28 = (f32[8,128]{1,0:T(8,128)S(1)}, s32[512]{0:T(512)S(4)}) custom-call(s32[512]{0:T(512)S(1)} %copy-done, f32[1024,128]{1,0:T(8,128)S(1)} %bitcast.21), custom_call_target="tpu_custom_call" | custom-call | flops 20000000 | bytes 600000 | tf_op jit(solution)/shard_map/pallas_call | solution.py:131
  33.0 2.0 %collective-permute-done = f32[192,2,128]{2,0,1:T(8,128)S(1)} collective-permute-done((f32[192,2,128]{2,0,1:T(8,128)S(1)}, f32[192,2,128]{2,0,1:T(8,128)S(1)}, u32[]{:S(2)}, u32[]{:S(2)}) %collective-permute-start) | collective-permute-done | bytes 196640 | tf_op jit(solution)/shard_map/ppermute | solution.py:124
  35.0 1.6 %shard_map.29 = f32[256,128]{1,0:T(8,128)S(1)} custom-call(s32[512]{0:T(512)S(4)} %get-tuple-element.7.offs_ref, s32[1]{0:T(128)} %bitcast.3.more_ref, f32[1024,128]{1,0:T(8,128)S(1)} %bitcast.22, f32[384,128]{1,0:T(8,128)S(1)} %bitcast.24, f32[8,128]{1,0:T(8,128)S(1)} %get-tuple-element.8.near_ref), custom_call_target="tpu_custom_call" | custom-call | flops 20000000 | bytes 600000 | tf_op jit(solution)/shard_map/pallas_call | solution.py:140
  36.6 12.9 %all_to_all.18 = f32[64,4,128]{2,1,0:T(4,128)S(1)} all-to-all(f32[64,4,128]{2,1,0:T(4,128)S(1)} %bitcast.23), channel_id=1, replica_groups={{168,184,188,172,236,252,248,232,40,104,100,36,52,48,32,96,112,116,120,..., dimensions={0} | all-to-all | bytes 262144 | tf_op jit(solution)/shard_map/all_to_all | solution.py:151
  49.5 0.0 collective-permute-start.1
  49.5 1.3 %collective-permute-done.1 = f32[256,128]{1,0:T(8,128)S(1)} collective-permute-done((f32[256,128]{1,0:T(8,128)S(1)}, f32[256,128]{1,0:T(8,128)S(1)}, u32[]{:S(2)}, u32[]{:S(2)}) %collective-permute-start.1) | collective-permute-done | bytes 131104 | tf_op jit(solution)/shard_map/ppermute | solution.py:152
  50.9 0.1 fusion.1
  51.0 0.8 %fusion = f32[64,2,4,128]{3,2,1,0:T(4,128)} fusion(f32[64,1,4,128]{3,2,1,0:T(4,128)S(1)} %get-tuple-element.10, f32[64,1,4,128]{3,2,1,0:T(4,128)S(1)} %get-tuple-element.9, f32[56,2,4,128]{3,2,1,0:T(4,128)S(1)} %fusion.1), kind=kLoop, calls=%fused_computation.1 | loop fusion | flops 131072 | bytes 753664 | tf_op jit(solution)/shard_map/jit(_roll_static)/concatenate | solution.py:158
  (3 shorter events, 0.1 us)
Async XLA Ops:
  29.8 5.2 %collective-permute-start = (f32[192,2,128]{2,0,1:T(8,128)S(1)}, f32[192,2,128]{2,0,1:T(8,128)S(1)}, u32[]{:S(2)}, u32[]{:S(2)}) collective-permute-start(f32[192,2,128]{2,0,1:T(8,128)S(1)} %pad_maximum_fusion.1), channel_id=1, source_target_pairs={{40,235},{42,40},{104,42},{106,104},{100,106},{102,100},{36,102},{... | collective-permute-start | bytes 589832 | tf_op jit(solution)/shard_map/ppermute | solution.py:124
  30.3 0.7 %copy-start = (s32[512]{0:T(512)S(1)}, s32[512]{0:T(512)}, u32[]{:S(2)}) copy-start(s32[512]{0:T(512)} %table_ref.1) | copy-start | bytes 6148
  49.5 1.3 %collective-permute-start.1 = (f32[256,128]{1,0:T(8,128)S(1)}, f32[256,128]{1,0:T(8,128)S(1)}, u32[]{:S(2)}, u32[]{:S(2)}) collective-permute-start(f32[256,128]{1,0:T(8,128)S(1)} %bitcast.27), channel_id=1, source_target_pairs={{0,2},{2,0},{4,6},{6,4},{8,10},{10,8},{12,14},{14,12},{16,18},{18,... | collective-permute-start | bytes 393224 | tf_op jit(solution)/shard_map/ppermute | solution.py:152

commit v10 on v9

--- a/solution.py
+++ b/solution.py
@@ -10,12 +10,12 @@
 LANES = 128
 VMEM_LIMIT = 6 * 2**20
 CHIPS = (
-    10, 26, 25, 9, 13, 12, 8, 24, 28, 29, 30, 14, 15, 31, 27, 11,
-    7, 3, 19, 18, 17, 21, 5, 4, 20, 16, 0, 1, 2, 6, 22, 23,
-    39, 35, 34, 38, 54, 55, 51, 50, 49, 53, 52, 48, 32, 33, 37, 36,
-    40, 56, 60, 44, 45, 61, 57, 41, 42, 46, 47, 43, 59, 63, 62, 58,
+    10, 11, 15, 31, 27, 23, 19, 18, 2, 3, 7, 6, 22, 26, 30, 14,
+    13, 12, 8, 4, 0, 16, 20, 24, 28, 29, 25, 9, 5, 1, 17, 21,
+    37, 33, 49, 53, 52, 48, 32, 36, 40, 56, 60, 44, 45, 61, 62, 63,
+    59, 55, 51, 35, 34, 50, 54, 38, 39, 43, 47, 46, 42, 41, 57, 58,
 )
-LEAD = 56
+LEAD = 60
 
 
 def sublanes():

time: 52 us -> 52.1 us (level)
  no operation moved by 1% of the time
where the time goes in v10:
time: 52.1 us; the launch traced here: 51.9 us
  blocking collectives  42.7 us (82%)
  Pallas kernels  3.63 us (7%)
  waiting for transfers between devices  3.17 us (6%)
  local copies, waits for them, and re-layouts  0.88 us (2%)
  other arithmetic  0.88 us (2%)
  starting transfers between devices  0.62 us (1%)
    all_to_all x1, blocking collectives, local(): lax.all_to_all(tiles, 'tm', 0, 0, axis_index_groups=[order], tiled=True)  29.7 us
    all_to_all x1, blocking collectives, local(): ours = lax.all_to_all(best, 'tm', 0, 0, axis_index_groups=cores, tiled=True)  13 us
    pallas_call x1, Pallas kernels, local(): pl.pallas_call(functools.partial(near_kernel, total, spot), out_shape=(ja...  2.04 us
    ppermute x1, waiting for transfers between devices, local(): halo = lax.ppermute(edge, ('tm', 'chan'), to_previous(order, groups))  1.93 us
    pallas_call x1, Pallas kernels, local(): pl.pallas_call(functools.partial(far_kernel, total, count // 2, spot), ou...  1.59 us
    ppermute x1, waiting for transfers between devices, local(): theirs = lax.ppermute(ours, 'tm', [(t, t ^ 1) for t in range(count)])  1.24 us
  transfers between devices with their start and end apart: 2, of which 2 were waited for; matrix products, arithmetic and copies ran while one was open for 0% of the time, Pallas kernels for 4%

profile of v10, /device:TPU:1, one launch (start us, length us, event | category | flops | bytes accessed | tf_op | source)
XLA Modules:
  0.0 51.9 jit_solution(10544553937558951263)
XLA Ops:
  0.0 29.7 %all_to_all.17 = f32[512,2,128]{2,1,0:T(2,128)S(1)} all-to-all(f32[512,2,128]{2,1,0:T(2,128)} %bitcast.29), channel_id=1, replica_groups={{40,42,44,46,60,62,124,126,108,110,92,94,76,78,72,74,8,10,12,14,28,30,2..., dimensions={0} | all-to-all | bytes 1048576 | tf_op jit(solution)/shard_map/all_to_all | solution.py:119
  29.7 0.1 slice.18
  29.8 0.1 slice.19
  29.9 0.5 collective-permute-start
  30.4 0.0 copy-start
  30.5 0.7 %copy-done = s32[512]{0:T(512)S(1)} copy-done((s32[512]{0:T(512)S(1)}, s32[512]{0:T(512)}, u32[]{:S(2)}) %copy-start) | copy-done | bytes 2072
  31.1 2.0 %shard_map.28 = (f32[8,128]{1,0:T(8,128)S(1)}, s32[512]{0:T(512)S(4)}) custom-call(s32[512]{0:T(512)S(1)} %copy-done, f32[1024,128]{1,0:T(8,128)S(1)} %bitcast.21), custom_call_target="tpu_custom_call" | custom-call | flops 20000000 | bytes 600000 | tf_op jit(solution)/shard_map/pallas_call | solution.py:131
  33.2 1.9 %collective-permute-done = f32[192,2,128]{2,0,1:T(8,128)S(1)} collective-permute-done((f32[192,2,128]{2,0,1:T(8,128)S(1)}, f32[192,2,128]{2,0,1:T(8,128)S(1)}, u32[]{:S(2)}, u32[]{:S(2)}) %collective-permute-start) | collective-permute-done | bytes 196640 | tf_op jit(solution)/shard_map/ppermute | solution.py:124
  35.1 1.6 %shard_map.29 = f32[256,128]{1,0:T(8,128)S(1)} custom-call(s32[512]{0:T(512)S(4)} %get-tuple-element.7.offs_ref, s32[1]{0:T(128)} %bitcast.3.more_ref, f32[1024,128]{1,0:T(8,128)S(1)} %bitcast.22, f32[384,128]{1,0:T(8,128)S(1)} %bitcast.24, f32[8,128]{1,0:T(8,128)S(1)} %get-tuple-element.8.near_ref), custom_call_target="tpu_custom_call" | custom-call | flops 20000000 | bytes 600000 | tf_op jit(solution)/shard_map/pallas_call | solution.py:140
  36.7 13.0 %all_to_all.18 = f32[64,4,128]{2,1,0:T(4,128)S(1)} all-to-all(f32[64,4,128]{2,1,0:T(4,128)S(1)} %bitcast.23), channel_id=1, replica_groups={{168,164,228,232,40,44,60,124,108,92,76,72,8,12,28,24,88,104,120,56,52,..., dimensions={0} | all-to-all | bytes 262144 | tf_op jit(solution)/shard_map/all_to_all | solution.py:151
  49.7 0.1 collective-permute-start.1
  49.8 1.2 %collective-permute-done.1 = f32[256,128]{1,0:T(8,128)S(1)} collective-permute-done((f32[256,128]{1,0:T(8,128)S(1)}, f32[256,128]{1,0:T(8,128)S(1)}, u32[]{:S(2)}, u32[]{:S(2)}) %collective-permute-start.1) | collective-permute-done | bytes 131104 | tf_op jit(solution)/shard_map/ppermute | solution.py:152
  51.1 0.1 fusion.1
  51.1 0.8 %fusion = f32[64,2,4,128]{3,2,1,0:T(4,128)} fusion(f32[64,1,4,128]{3,2,1,0:T(4,128)S(1)} %get-tuple-element.10, f32[64,1,4,128]{3,2,1,0:T(4,128)S(1)} %get-tuple-element.9, f32[60,2,4,128]{3,2,1,0:T(4,128)S(1)} %fusion.1), kind=kLoop, calls=%fused_computation.1 | loop fusion | flops 131072 | bytes 770048 | tf_op jit(solution)/shard_map/jit(_roll_static)/concatenate | solution.py:158
  (3 shorter events, 0.1 us)
Async XLA Ops:
  29.9 5.2 %collective-permute-start = (f32[192,2,128]{2,0,1:T(8,128)S(1)}, f32[192,2,128]{2,0,1:T(8,128)S(1)}, u32[]{:S(2)}, u32[]{:S(2)}) collective-permute-start(f32[192,2,128]{2,0,1:T(8,128)S(1)} %pad_maximum_fusion.1), channel_id=1, source_target_pairs={{40,235},{42,40},{44,42},{46,44},{60,46},{62,60},{124,62},{126,124... | collective-permute-start | bytes 589832 | tf_op jit(solution)/shard_map/ppermute | solution.py:124
  30.4 0.7 %copy-start = (s32[512]{0:T(512)S(1)}, s32[512]{0:T(512)}, u32[]{:S(2)}) copy-start(s32[512]{0:T(512)} %table_ref.1) | copy-start | bytes 6148
  49.7 1.3 %collective-permute-start.1 = (f32[256,128]{1,0:T(8,128)S(1)}, f32[256,128]{1,0:T(8,128)S(1)}, u32[]{:S(2)}, u32[]{:S(2)}) collective-permute-start(f32[256,128]{1,0:T(8,128)S(1)} %bitcast.27), channel_id=1, source_target_pairs={{0,2},{2,0},{4,6},{6,4},{8,10},{10,8},{12,14},{14,12},{16,18},{18,... | collective-permute-start | bytes 393224 | tf_op jit(solution)/shard_map/ppermute | solution.py:152
